TPU v7x, 32 devices: a whole 2x2x4 slice. The times are simulated.
32 devices in a mesh: rep: 2 (over x), dp: 16 (over y, z, core).
Axes of the slice: x: 2, y: 2, z: 4, core: 2. Of those that a mesh axis runs over, the one named last changes fastest.
Arguments:
- x: bfloat16 [32, 2048, 896], P(('rep', 'dp')), parts along dimension 0
- dy: bfloat16 [32, 2048, 896], P(('rep', 'dp')), parts along dimension 0
- w_gate: bfloat16 [2, 896, 2560], replicated
- w_up: bfloat16 [2, 896, 2560], replicated
- w_down: bfloat16 [2, 2560, 896], replicated
- m_w_gate: float32 [2, 896, 2560], P(None, 'dp')
- m_w_up: float32 [2, 896, 2560], P(None, 'dp')
- m_w_down: float32 [2, 2560, 896], P(None, 'dp')
- v_w_gate: float32 [2, 896, 2560], P(None, 'dp')
- v_w_up: float32 [2, 896, 2560], P(None, 'dp')
- v_w_down: float32 [2, 2560, 896], P(None, 'dp')
Outputs:
- output 1: bfloat16 [4, 896, 2560], P('rep'), parts along dimension 0
- output 2: bfloat16 [4, 896, 2560], P('rep'), parts along dimension 0
- output 3: bfloat16 [4, 2560, 896], P('rep'), parts along dimension 0
- output 4: float32 [4, 896, 2560], P('rep', 'dp'), parts along dimension 0
- output 5: float32 [4, 896, 2560], P('rep', 'dp'), parts along dimension 0
- output 6: float32 [4, 2560, 896], P('rep', 'dp'), parts along dimension 0
- output 7: float32 [4, 896, 2560], P('rep', 'dp'), parts along dimension 0
- output 8: float32 [4, 896, 2560], P('rep', 'dp'), parts along dimension 0
- output 9: float32 [4, 2560, 896], P('rep', 'dp'), parts along dimension 0
There are 2 independent parts. A program takes and returns all parts, laid end to end along the dimension named above; an argument that names none is the same for every part.
All inputs are finite; a program needn't handle non-finite values.
Results may differ from a plain program's by a relative error of at most 0.022.
Values are sent between devices in bfloat16 or wider.
A program may use at most 2 GiB of HBM per device.

v0:
```python
import jax
import jax.numpy as jnp
from jax import lax

NAMES = ("w_gate", "w_up", "w_down")


def matmul(a, w):
    return jnp.dot(a, w, preferred_element_type=jnp.float32).astype(jnp.bfloat16)


def normed(h):
    wide = h.astype(jnp.float32)
    scale = lax.rsqrt(jnp.mean(wide**2, -1, keepdims=True) + 1e-6)
    return (wide * scale).astype(jnp.bfloat16)


def layer(h, w):
    a = normed(h)
    gate = jnp.dot(a, w["w_gate"], preferred_element_type=jnp.float32)
    up = jnp.dot(a, w["w_up"], preferred_element_type=jnp.float32)
    return h + matmul((jax.nn.silu(gate) * up).astype(jnp.bfloat16), w["w_down"])


def adamw(w, m, v, g):
    m = 0.9 * m + 0.1 * g
    v = 0.95 * v + 0.05 * g * g
    step = m * lax.rsqrt(v + 1e-8) + 0.1 * w
    return (w - 0.02 * step).astype(jnp.bfloat16), m, v


def stack(weights, h):
    for number in range(weights["w_gate"].shape[0]):
        h = layer(h, {name: w[number] for name, w in weights.items()})
    return h


def solution(mesh):
    groups = mesh.shape["rep"]

    def step(x, dy, *arrays):
        weights, m, v = (arrays[i : i + 3] for i in (0, 3, 6))
        x, dy = (t.reshape(groups, -1, *t.shape[1:]) for t in (x, dy))

        def of_a_group(x, dy):
            _, back = jax.vjp(lambda w: stack(w, x), dict(zip(NAMES, weights, strict=True)))
            by_weights = back(dy)[0]
            gradients = [by_weights[name].astype(jnp.float32) for name in NAMES]
            new = [adamw(w.astype(jnp.float32), m, v, g) for w, m, v, g in zip(weights, m, v, gradients, strict=True)]
            return tuple(one[which] for which in range(3) for one in new)

        return tuple(t.reshape(-1, *t.shape[2:]) for t in jax.vmap(of_a_group)(x, dy))

    return step
```

profile of v0, /device:TPU:0, one launch (start us, length us, event | category | flops | bytes accessed | tf_op | source)
XLA Modules:
  0.0 1359.7 jit_solution(4869622746577915156)
XLA Ops:
  21.3 17.1 %fusion.180 = f32[2048,2560]{1,0:T(8,128)} fusion(bf16[2,896,2560]{2,1,0:T(8,128)(2,1)} %param.12, bf16[1,2048,896]{2,1,0:T(8,128)(2,1)S(1)} %copy-done.11, f32[2048]{0:T(1024)S(1)} %add_rsqrt_fusion), kind=kOutput, calls=%fused_computation.228 | convolution fusion | flops 9400745984 | bytes 29237248 | tf_op jit(solution)/vmap(jvp())/dot_general | solution.py:20
  38.4 24.5 %fusion.156 = (bf16[1,1,2048,2560]{3,2,1,0:T(8,128)(2,1)}, f32[2048,2560]{1,0:T(8,128)}) fusion(f32[2048,2560]{1,0:T(8,128)} %fusion.180, bf16[2,896,2560]{2,1,0:T(8,128)(2,1)} %param.15, bf16[1,2048,896]{2,1,0:T(8,128)(2,1)S(1)} %copy-done.11, f32[2048]{0:T(1024)S(1)} %add_rsqrt_fusion), kind=kOutput, calls=%fused_computation.191 | convolution fusion | flops 9432203264 | bytes 60694528 | tf_op jit(solution)/vmap(jvp())/dot_general | solution.py:21
  62.9 15.9 %fusion.166 = (f32[2048]{0:T(1024)S(1)}, bf16[1,1,2048,896]{2,3,1,0:T(8,128)(2,1)}) fusion(bf16[2,2560,896]{2,1,0:T(8,128)(2,1)} %param.16, bf16[1,1,2048,2560]{3,2,1,0:T(8,128)(2,1)} %get-tuple-element.263, bf16[1,2048,896]{1,2,0:T(8,128)(2,1)S(1)} %copy-done.13), kind=kOutput, calls=%fused_computation.213 | convolution fusion | flops 9404413952 | bytes 22421504 | tf_op jit(solution)/vmap(jvp())/dot_general | solution.py:9
  82.4 18.5 %fusion.169 = f32[2048,2560]{1,0:T(8,128)} fusion(bf16[2,896,2560]{2,1,0:T(8,128)(2,1)} %param.12, bf16[1,1,2048,896]{2,3,1,0:T(8,128)(2,1)S(1)} %fusion.167), kind=kOutput, calls=%fused_computation.217 | convolution fusion | flops 9395240960 | bytes 29229056 | tf_op jit(solution)/vmap(jvp())/dot_general | solution.py:20
  101.0 24.6 %fusion.155 = (bf16[1,1,2048,2560]{3,2,1,0:T(8,128)(2,1)}, f32[2048,2560]{1,0:T(8,128)}) fusion(f32[2048,2560]{1,0:T(8,128)} %fusion.169, bf16[2,896,2560]{2,1,0:T(8,128)(2,1)} %param.15, bf16[1,1,2048,896]{2,3,1,0:T(8,128)(2,1)S(1)} %fusion.167), kind=kOutput, calls=%fused_computation.189 | convolution fusion | flops 9426698240 | bytes 60686336 | tf_op jit(solution)/vmap(jvp())/dot_general | solution.py:21
  131.7 27.6 %convert_multiply_fusion.2 = (bf16[1,1,2048,2560]{3,2,1,0:T(8,128)(2,1)S(1)}, bf16[1,1,2048,2560]{3,2,1,0:T(8,128)(2,1)}) fusion(f32[2048,2560]{1,0:T(8,128)} %fusion.169, f32[2048,2560]{1,0:T(8,128)} %get-tuple-element.270, bf16[2,2560,896]{2,1,0:T(8,128)(2,1)} %param.16, bf16[1,2048,896]{2,1,0:T(8,128)(2,1)} %param.17), kind=kOutput, calls=%fused_computation.172 | convolution fusion | flops 9479127040 | bytes 71172096 | tf_op jit(solution)/vmap(transpose(jvp()))/dot_general | solution.py:9
  159.3 18.8 %fusion.148 = bf16[2048,896]{0,1:T(8,128)(2,1)} fusion(bf16[1,1,2048,2560]{3,2,1,0:T(8,128)(2,1)} %get-tuple-element.545, bf16[2,896,2560]{2,1,0:T(8,128)(2,1)} %param.12), kind=kOutput, calls=%fused_computation.178 | convolution fusion | flops 9395240960 | bytes 18743296 | tf_op jit(solution)/vmap(transpose(jvp()))/dot_general | solution.py:20
  178.1 14.2 %fusion.168 = (f32[2048]{0:T(1024)S(1)}, bf16[2048,896]{0,1:T(8,128)(2,1)}) fusion(bf16[1,1,2048,896]{2,3,1,0:T(8,128)(2,1)S(1)} %copy-done.14, bf16[2048,896]{0,1:T(8,128)(2,1)} %fusion.148, bf16[2,896,2560]{2,1,0:T(8,128)(2,1)} %param.15, bf16[1,1,2048,2560]{3,2,1,0:T(8,128)(2,1)S(1)} %get-tuple-element.623), kind=kOutput, calls=%fused_computation.215 | convolution fusion | flops 9404413952 | bytes 26091520 | tf_op jit(solution)/vmap(transpose(jvp()))/dot_general | solution.py:21
  199.3 29.5 %convert_multiply_fusion = (bf16[1,1,2048,2560]{3,2,1,0:T(8,128)(2,1)}, bf16[1,1,2048,2560]{3,2,1,0:T(8,128)(2,1)}) fusion(f32[2048,2560]{1,0:T(8,128)} %fusion.180, f32[2048,2560]{1,0:T(8,128)} %get-tuple-element.264, bf16[2,2560,896]{2,1,0:T(8,128)(2,1)} %param.16, bf16[1,1,2048,896]{2,3,1,0:T(8,128)(2,1)S(1)} %fusion.191), kind=kOutput, calls=%fused_computation.170 | convolution fusion | flops 9479127040 | bytes 71172096 | tf_op jit(solution)/vmap(transpose(jvp()))/dot_general | solution.py:9
  228.8 137.1 %while.13 = (bf16[1,1,2048,896]{2,3,1,0:T(8,128)(2,1)}, bf16[1,1,2048,2560]{3,2,1,0:T(8,128)(2,1)}, f32[1,56,2560]{2,1,0:T(8,128)S(1)}, f32[1,56,2560]{2,1,0:T(8...) while((bf16[1,1,2048,896]{2,3,1,0:T(8,128)(2,1)}, ...), condition=%wide.windowed_dot_general_cond_rs.1.clone, body=%wide.windowed_dot_general_body_rs.1.clone.sunk | while | flops 2351505408 | bytes 105579168 | solution.py:20
  251.9 9.0 collective-permute-done.6
  284.1 11.2 collective-permute-done.6
  319.8 10.3 collective-permute-done.6
  353.4 11.6 collective-permute-done.6
  365.9 143.0 %while.12 = (bf16[1,1,2048,896]{2,3,1,0:T(8,128)(2,1)}, bf16[1,1,2048,2560]{3,2,1,0:T(8,128)(2,1)}, f32[1,56,2560]{2,1,0:T(8,128)S(1)}, f32[1,56,2560]{2,1,0:T(8...) while((bf16[1,1,2048,896]{2,3,1,0:T(8,128)(2,1)}, ...), condition=%wide.windowed_dot_general_cond_rs.clone, body=%wide.windowed_dot_general_body_rs.clone.sunk | while | flops 2351505408 | bytes 105579168 | solution.py:20
  379.2 10.9 collective-permute-done
  430.5 10.2 collective-permute-done.2
  466.3 8.6 collective-permute-done.2
  499.9 8.0 collective-permute-done.2
  509.0 143.1 %while.15 = (bf16[1,1,2048,896]{2,3,1,0:T(8,128)(2,1)}, bf16[1,1,2048,2560]{3,2,1,0:T(8,128)(2,1)}, f32[1,56,2560]{2,1,0:T(8,128)S(1)}, f32[1,56,2560]{2,1,0:T(8...) while((bf16[1,1,2048,896]{2,3,1,0:T(8,128)(2,1)}, ...), condition=%wide.windowed_dot_general_cond_rs.3.clone, body=%wide.windowed_dot_general_body_rs.3.clone.sunk | while | flops 2351505408 | bytes 105579168 | solution.py:21
  522.2 10.9 collective-permute-done.12
  572.5 8.8 collective-permute-done.14
  605.4 8.8 collective-permute-done.14
  640.9 10.2 collective-permute-done.14
  659.8 186.9 %while.14 = (bf16[1,1,2048,896]{2,3,1,0:T(8,128)(2,1)}, bf16[1,1,2048,2560]{3,2,1,0:T(8,128)(2,1)}, f32[1,56,2560]{2,1,0:T(8,128)S(1)}, f32[1,56,2560]{2,1,0:T(8...) while((bf16[1,1,2048,896]{2,3,1,0:T(8,128)(2,1)}, ...), condition=%wide.windowed_dot_general_cond_rs.2.clone, body=%wide.windowed_dot_general_body_rs.2.clone.sunk | while | flops 2351505408 | bytes 105579168 | solution.py:21
  677.3 14.0 %collective-permute-start.10 = (f32[1,56,2560]{2,1,0:T(8,128)S(1)}, f32[1,56,2560]{2,1,0:T(8,128)S(1)}, u32[]{:S(2)}, u32[]{:S(2)}) collective-permute-start(f32[1,56,2560]{2,1,0:T(8,128)S(1)} %get-tuple-element.474), channel_id=18, source_target_pairs={{0,1},{1,2},{2,3},{3,4},{4,5},{5,6},{6,7},{7,8},{8,9},{9,10},{10,1... | collective-permute-start | bytes 1720328 | tf_op jit(solution)/vmap(transpose(jvp()))/dot_general | solution.py:21
  693.8 18.7 %collective-permute-done.11 = f32[1,56,2560]{2,1,0:T(8,128)S(1)} collective-permute-done((f32[1,56,2560]{2,1,0:T(8,128)S(1)}, f32[1,56,2560]{2,1,0:T(8,128)S(1)}, u32[]{:S(2)}, u32[]{:S(2)}) %collective-permute-start.11) | collective-permute-done | bytes 573472 | tf_op jit(solution)/vmap(transpose(jvp()))/dot_general | solution.py:21
  712.6 8.4 collective-permute-start.8
  741.4 22.7 %collective-permute-done.10 = f32[1,56,2560]{2,1,0:T(8,128)S(1)} collective-permute-done((f32[1,56,2560]{2,1,0:T(8,128)S(1)}, f32[1,56,2560]{2,1,0:T(8,128)S(1)}, u32[]{:S(2)}, u32[]{:S(2)}) %collective-permute-start.10) | collective-permute-done | bytes 573472 | tf_op jit(solution)/vmap(transpose(jvp()))/dot_general | solution.py:21
  764.5 14.3 %collective-permute-start.8 = (f32[1,56,2560]{2,1,0:T(8,128)S(1)}, f32[1,56,2560]{2,1,0:T(8,128)S(1)}, u32[]{:S(2)}, u32[]{:S(2)}) collective-permute-start(f32[1,56,2560]{2,1,0:T(8,128)S(1)} %broadcast_select_fusion.28), channel_id=16, source_target_pairs={{0,1},{1,2},{2,3},{3,4},{4,5},{5,6},{6,7},{7,8},{8,9},{9,10},{10,1... | collective-permute-start | bytes 1720328 | tf_op jit(solution)/vmap(transpose(jvp()))/dot_general | solution.py:21
  804.3 11.1 collective-permute-done.10
  838.5 8.1 collective-permute-done.10
  847.9 10.7 collective-permute-done.26
  862.7 14.5 %copy.4 = bf16[1,1,2048,2560]{2,3,1,0:T(8,128)(2,1)} copy(bf16[1,1,2048,2560]{3,2,1,0:T(8,128)(2,1)} %get-tuple-element.263) | data formatting | bytes 20971520
  883.3 187.3 %while.17 = (bf16[1,1,2048,2560]{2,3,1,0:T(8,128)(2,1)}, bf16[1,1,2048,896]{3,2,1,0:T(8,128)(2,1)}, f32[1,160,896]{2,1,0:T(8,128)S(1)}, f32[1,160,896]{2,1,0:T(8...) while((bf16[1,1,2048,2560]{2,3,1,0:T(8,128)(2,1)}, ...), condition=%wide.windowed_dot_general_cond_rs.5.clone, body=%wide.windowed_dot_general_body_rs.5.clone.sunk | while | flops 2354913280 | bytes 48956004 | solution.py:9
  893.7 16.8 %collective-permute-done.20 = f32[1,160,896]{2,1,0:T(8,128)S(1)} collective-permute-done((f32[1,160,896]{2,1,0:T(8,128)S(1)}, f32[1,160,896]{2,1,0:T(8,128)S(1)}, u32[]{:S(2)}, u32[]{:S(2)}) %collective-permute-start.20) | collective-permute-done | bytes 573472 | tf_op jit(solution)/vmap(transpose(jvp()))/dot_general | solution.py:9
  919.8 13.7 %collective-permute-done.22 = f32[1,160,896]{2,1,0:T(8,128)S(1)} collective-permute-done((f32[1,160,896]{2,1,0:T(8,128)S(1)}, f32[1,160,896]{2,1,0:T(8,128)S(1)}, u32[]{:S(2)}, u32[]{:S(2)}) %collective-permute-start.22) | collective-permute-done | bytes 573472 | tf_op jit(solution)/vmap(transpose(jvp()))/dot_general | solution.py:9
  938.0 18.9 %collective-permute-start.20 = (f32[1,160,896]{2,1,0:T(8,128)S(1)}, f32[1,160,896]{2,1,0:T(8,128)S(1)}, u32[]{:S(2)}, u32[]{:S(2)}) collective-permute-start(f32[1,160,896]{2,1,0:T(8,128)S(1)} %broadcast_select_fusion.34), channel_id=35, source_target_pairs={{0,1},{1,2},{2,3},{3,4},{4,5},{5,6},{6,7},{7,8},{8,9},{9,10},{10,1... | collective-permute-start | bytes 1720328 | tf_op jit(solution)/vmap(transpose(jvp()))/dot_general | solution.py:9
  976.0 8.6 collective-permute-start.22
  1061.4 8.2 collective-permute-done.22
  1070.8 14.5 %copy.2 = bf16[1,1,2048,2560]{2,3,1,0:T(8,128)(2,1)} copy(bf16[1,1,2048,2560]{3,2,1,0:T(8,128)(2,1)} %get-tuple-element.269) | data formatting | bytes 20971520
  1091.4 146.4 %while.16 = (bf16[1,1,2048,2560]{2,3,1,0:T(8,128)(2,1)}, bf16[1,1,2048,896]{3,2,1,0:T(8,128)(2,1)}, f32[1,160,896]{2,1,0:T(8,128)S(1)}, f32[1,160,896]{2,1,0:T(8...) while((bf16[1,1,2048,2560]{2,3,1,0:T(8,128)(2,1)}, ...), condition=%wide.windowed_dot_general_cond_rs.4.clone, body=%wide.windowed_dot_general_body_rs.4.clone.sunk | while | flops 2354913280 | bytes 48956004 | solution.py:9
  1117.4 8.2 collective-permute-done.18
  1154.5 8.6 collective-permute-done.18
  1191.4 8.5 collective-permute-done.18
  1228.2 8.6 collective-permute-done.18
  1238.9 10.7 collective-permute-done.28
  1253.7 75.3 %all-gather.14.cloned.1.call-done = bf16[1,2,2560,896]{3,2,1,0:T(8,128)(2,1)} async-done(((bf16[1,2,160,896]{3,2,1,0:T(8,128)(2,1)}), bf16[1,2,2560,896]{3,2,1,0:T(8,128)(2,1)}) %all-gather.14.cloned.1.call-update) | async-done | bytes 9175056 | tf_op jit(solution)/reshape | solution.py:52
  (475 shorter events, 663.6 us)
Async XLA Ops:
  7.2 1246.5 %all-gather.10.cloned.1.call-start = ((), (), s32[]{:S(2)}) async-start(), calls=%async_computation | async-start | bytes 9748480 | tf_op jit(solution)/reshape | solution.py:52
  277.9 17.4 %collective-permute-start.6 = (f32[1,56,2560]{2,1,0:T(8,128)S(1)}, f32[1,56,2560]{2,1,0:T(8,128)S(1)}, u32[]{:S(2)}, u32[]{:S(2)}) collective-permute-start(f32[1,56,2560]{2,1,0:T(8,128)S(1)} %get-tuple-element.465), channel_id=11, source_target_pairs={{0,1},{1,2},{2,3},{3,4},{4,5},{5,6},{6,7},{7,8},{8,9},{9,10},{10,1... | collective-permute-start | bytes 1720328 | tf_op jit(solution)/vmap(transpose(jvp()))/dot_general | solution.py:20
  278.0 17.3 %collective-permute-start.7 = (f32[1,56,2560]{2,1,0:T(8,128)S(1)}, f32[1,56,2560]{2,1,0:T(8,128)S(1)}, u32[]{:S(2)}, u32[]{:S(2)}) collective-permute-start(f32[1,56,2560]{2,1,0:T(8,128)S(1)} %get-tuple-element.466), channel_id=10, source_target_pairs={{0,15},{1,0},{2,1},{3,2},{4,3},{5,4},{6,5},{7,6},{8,7},{9,8},{10,9... | collective-permute-start | bytes 1720328 | tf_op jit(solution)/vmap(transpose(jvp()))/dot_general | solution.py:20
  347.1 17.9 %collective-permute-start.6 = (f32[1,56,2560]{2,1,0:T(8,128)S(1)}, f32[1,56,2560]{2,1,0:T(8,128)S(1)}, u32[]{:S(2)}, u32[]{:S(2)}) collective-permute-start(f32[1,56,2560]{2,1,0:T(8,128)S(1)} %get-tuple-element.465), channel_id=11, source_target_pairs={{0,1},{1,2},{2,3},{3,4},{4,5},{5,6},{6,7},{7,8},{8,9},{9,10},{10,1... | collective-permute-start | bytes 1720328 | tf_op jit(solution)/vmap(transpose(jvp()))/dot_general | solution.py:20
  347.2 17.8 %collective-permute-start.7 = (f32[1,56,2560]{2,1,0:T(8,128)S(1)}, f32[1,56,2560]{2,1,0:T(8,128)S(1)}, u32[]{:S(2)}, u32[]{:S(2)}) collective-permute-start(f32[1,56,2560]{2,1,0:T(8,128)S(1)} %get-tuple-element.466), channel_id=10, source_target_pairs={{0,15},{1,0},{2,1},{3,2},{4,3},{5,4},{6,5},{7,6},{8,7},{9,8},{10,9... | collective-permute-start | bytes 1720328 | tf_op jit(solution)/vmap(transpose(jvp()))/dot_general | solution.py:20
  365.9 287.6 %collective-permute-start.25 = (f32[1,56,2560]{2,1,0:T(8,128)}, f32[1,56,2560]{2,1,0:T(8,128)}, u32[]{:S(2)}, u32[]{:S(2)}) collective-permute-start(f32[1,56,2560]{2,1,0:T(8,128)} %get-tuple-element.39), channel_id=12, source_target_pairs={{0,1},{1,2},{2,3},{3,4},{4,5},{5,6},{6,7},{7,8},{8,9},{9,10},{10,1... | collective-permute-start | bytes 1720328 | tf_op jit(solution)/vmap(transpose(jvp()))/dot_general | solution.py:20
  366.0 24.1 %collective-permute-start = (f32[1,56,2560]{2,1,0:T(8,128)S(1)}, f32[1,56,2560]{2,1,0:T(8,128)S(1)}, u32[]{:S(2)}, u32[]{:S(2)}) collective-permute-start(f32[1,56,2560]{2,1,0:T(8,128)S(1)} %broadcast_select_fusion.24), channel_id=3, source_target_pairs={{0,1},{1,2},{2,3},{3,4},{4,5},{5,6},{6,7},{7,8},{8,9},{9,10},{10,1... | collective-permute-start | bytes 1720328 | tf_op jit(solution)/vmap(transpose(jvp()))/dot_general | solution.py:20
  366.1 24.0 %collective-permute-start.1 = (f32[1,56,2560]{2,1,0:T(8,128)S(1)}, f32[1,56,2560]{2,1,0:T(8,128)S(1)}, u32[]{:S(2)}, u32[]{:S(2)}) collective-permute-start(f32[1,56,2560]{2,1,0:T(8,128)S(1)} %broadcast_select_fusion.25), channel_id=2, source_target_pairs={{0,15},{1,0},{2,1},{3,2},{4,3},{5,4},{6,5},{7,6},{8,7},{9,8},{10,9... | collective-permute-start | bytes 1720328 | tf_op jit(solution)/vmap(transpose(jvp()))/dot_general | solution.py:20
  406.6 17.4 %collective-permute-start = (f32[1,56,2560]{2,1,0:T(8,128)S(1)}, f32[1,56,2560]{2,1,0:T(8,128)S(1)}, u32[]{:S(2)}, u32[]{:S(2)}) collective-permute-start(f32[1,56,2560]{2,1,0:T(8,128)S(1)} %broadcast_select_fusion.24), channel_id=3, source_target_pairs={{0,1},{1,2},{2,3},{3,4},{4,5},{5,6},{6,7},{7,8},{8,9},{9,10},{10,1... | collective-permute-start | bytes 1720328 | tf_op jit(solution)/vmap(transpose(jvp()))/dot_general | solution.py:20
  406.7 17.3 %collective-permute-start.1 = (f32[1,56,2560]{2,1,0:T(8,128)S(1)}, f32[1,56,2560]{2,1,0:T(8,128)S(1)}, u32[]{:S(2)}, u32[]{:S(2)}) collective-permute-start(f32[1,56,2560]{2,1,0:T(8,128)S(1)} %broadcast_select_fusion.25), channel_id=2, source_target_pairs={{0,15},{1,0},{2,1},{3,2},{4,3},{5,4},{6,5},{7,6},{8,7},{9,8},{10,9... | collective-permute-start | bytes 1720328 | tf_op jit(solution)/vmap(transpose(jvp()))/dot_general | solution.py:20
  509.0 145.7 %collective-permute-start.24 = (f32[1,56,2560]{2,1,0:T(8,128)}, f32[1,56,2560]{2,1,0:T(8,128)}, u32[]{:S(2)}, u32[]{:S(2)}) collective-permute-start(f32[1,56,2560]{2,1,0:T(8,128)} %get-tuple-element.37), channel_id=6, source_target_pairs={{0,1},{1,2},{2,3},{3,4},{4,5},{5,6},{6,7},{7,8},{8,9},{9,10},{10,1... | collective-permute-start | bytes 1720328 | tf_op jit(solution)/vmap(transpose(jvp()))/dot_general | solution.py:20
  509.0 24.1 %collective-permute-start.12 = (f32[1,56,2560]{2,1,0:T(8,128)S(1)}, f32[1,56,2560]{2,1,0:T(8,128)S(1)}, u32[]{:S(2)}, u32[]{:S(2)}) collective-permute-start(f32[1,56,2560]{2,1,0:T(8,128)S(1)} %broadcast_select_fusion.30), channel_id=22, source_target_pairs={{0,1},{1,2},{2,3},{3,4},{4,5},{5,6},{6,7},{7,8},{8,9},{9,10},{10,1... | collective-permute-start | bytes 1720328 | tf_op jit(solution)/vmap(transpose(jvp()))/dot_general | solution.py:21
  509.1 24.0 %collective-permute-start.13 = (f32[1,56,2560]{2,1,0:T(8,128)S(1)}, f32[1,56,2560]{2,1,0:T(8,128)S(1)}, u32[]{:S(2)}, u32[]{:S(2)}) collective-permute-start(f32[1,56,2560]{2,1,0:T(8,128)S(1)} %broadcast_select_fusion.31), channel_id=21, source_target_pairs={{0,15},{1,0},{2,1},{3,2},{4,3},{5,4},{6,5},{7,6},{8,7},{9,8},{10,9... | collective-permute-start | bytes 1720328 | tf_op jit(solution)/vmap(transpose(jvp()))/dot_general | solution.py:21
  548.9 17.2 %collective-permute-start.12 = (f32[1,56,2560]{2,1,0:T(8,128)S(1)}, f32[1,56,2560]{2,1,0:T(8,128)S(1)}, u32[]{:S(2)}, u32[]{:S(2)}) collective-permute-start(f32[1,56,2560]{2,1,0:T(8,128)S(1)} %broadcast_select_fusion.30), channel_id=22, source_target_pairs={{0,1},{1,2},{2,3},{3,4},{4,5},{5,6},{6,7},{7,8},{8,9},{9,10},{10,1... | collective-permute-start | bytes 1720328 | tf_op jit(solution)/vmap(transpose(jvp()))/dot_general | solution.py:21
  617.1 17.4 %collective-permute-start.12 = (f32[1,56,2560]{2,1,0:T(8,128)S(1)}, f32[1,56,2560]{2,1,0:T(8,128)S(1)}, u32[]{:S(2)}, u32[]{:S(2)}) collective-permute-start(f32[1,56,2560]{2,1,0:T(8,128)S(1)} %broadcast_select_fusion.30), channel_id=22, source_target_pairs={{0,1},{1,2},{2,3},{3,4},{4,5},{5,6},{6,7},{7,8},{8,9},{9,10},{10,1... | collective-permute-start | bytes 1720328 | tf_op jit(solution)/vmap(transpose(jvp()))/dot_general | solution.py:21
  652.1 194.7 %collective-permute-start.27 = (f32[1,56,2560]{2,1,0:T(8,128)}, f32[1,56,2560]{2,1,0:T(8,128)}, u32[]{:S(2)}, u32[]{:S(2)}) collective-permute-start(f32[1,56,2560]{2,1,0:T(8,128)} %get-tuple-element.43), channel_id=25, source_target_pairs={{0,1},{1,2},{2,3},{3,4},{4,5},{5,6},{6,7},{7,8},{8,9},{9,10},{10,1... | collective-permute-start | bytes 1720328 | tf_op jit(solution)/vmap(transpose(jvp()))/dot_general | solution.py:21
  659.8 593.9 %all-gather.12.cloned.1.call-start = ((), (), s32[]{:S(2)}) async-start(), calls=%async_computation.1 | async-start | bytes 9748480 | tf_op jit(solution)/reshape | solution.py:52
  659.9 17.3 %collective-permute-start.8 = (f32[1,56,2560]{2,1,0:T(8,128)S(1)}, f32[1,56,2560]{2,1,0:T(8,128)S(1)}, u32[]{:S(2)}, u32[]{:S(2)}) collective-permute-start(f32[1,56,2560]{2,1,0:T(8,128)S(1)} %broadcast_select_fusion.28), channel_id=16, source_target_pairs={{0,1},{1,2},{2,3},{3,4},{4,5},{5,6},{6,7},{7,8},{8,9},{9,10},{10,1... | collective-permute-start | bytes 1720328 | tf_op jit(solution)/vmap(transpose(jvp()))/dot_general | solution.py:21
  660.0 17.2 %collective-permute-start.9 = (f32[1,56,2560]{2,1,0:T(8,128)S(1)}, f32[1,56,2560]{2,1,0:T(8,128)S(1)}, u32[]{:S(2)}, u32[]{:S(2)}) collective-permute-start(f32[1,56,2560]{2,1,0:T(8,128)S(1)} %broadcast_select_fusion.29), channel_id=15, source_target_pairs={{0,15},{1,0},{2,1},{3,2},{4,3},{5,4},{6,5},{7,6},{8,7},{9,8},{10,9... | collective-permute-start | bytes 1720328 | tf_op jit(solution)/vmap(transpose(jvp()))/dot_general | solution.py:21
  691.3 21.1 %collective-permute-start.11 = (f32[1,56,2560]{2,1,0:T(8,128)S(1)}, f32[1,56,2560]{2,1,0:T(8,128)S(1)}, u32[]{:S(2)}, u32[]{:S(2)}) collective-permute-start(f32[1,56,2560]{2,1,0:T(8,128)S(1)} %get-tuple-element.475), channel_id=17, source_target_pairs={{0,15},{1,0},{2,1},{3,2},{4,3},{5,4},{6,5},{7,6},{8,7},{9,8},{10,9... | collective-permute-start | bytes 1720328 | tf_op jit(solution)/vmap(transpose(jvp()))/dot_general | solution.py:21
  712.6 20.6 %collective-permute-start.8 = (f32[1,56,2560]{2,1,0:T(8,128)S(1)}, f32[1,56,2560]{2,1,0:T(8,128)S(1)}, u32[]{:S(2)}, u32[]{:S(2)}) collective-permute-start(f32[1,56,2560]{2,1,0:T(8,128)S(1)} %broadcast_select_fusion.28), channel_id=16, source_target_pairs={{0,1},{1,2},{2,3},{3,4},{4,5},{5,6},{6,7},{7,8},{8,9},{9,10},{10,1... | collective-permute-start | bytes 1720328 | tf_op jit(solution)/vmap(transpose(jvp()))/dot_general | solution.py:21
  734.9 29.2 %collective-permute-start.10 = (f32[1,56,2560]{2,1,0:T(8,128)S(1)}, f32[1,56,2560]{2,1,0:T(8,128)S(1)}, u32[]{:S(2)}, u32[]{:S(2)}) collective-permute-start(f32[1,56,2560]{2,1,0:T(8,128)S(1)} %get-tuple-element.474), channel_id=18, source_target_pairs={{0,1},{1,2},{2,3},{3,4},{4,5},{5,6},{6,7},{7,8},{8,9},{9,10},{10,1... | collective-permute-start | bytes 1720328 | tf_op jit(solution)/vmap(transpose(jvp()))/dot_general | solution.py:21
  736.2 28.1 %collective-permute-start.11 = (f32[1,56,2560]{2,1,0:T(8,128)S(1)}, f32[1,56,2560]{2,1,0:T(8,128)S(1)}, u32[]{:S(2)}, u32[]{:S(2)}) collective-permute-start(f32[1,56,2560]{2,1,0:T(8,128)S(1)} %get-tuple-element.475), channel_id=17, source_target_pairs={{0,15},{1,0},{2,1},{3,2},{4,3},{5,4},{6,5},{7,6},{8,7},{9,8},{10,9... | collective-permute-start | bytes 1720328 | tf_op jit(solution)/vmap(transpose(jvp()))/dot_general | solution.py:21
  764.5 30.2 %collective-permute-start.8 = (f32[1,56,2560]{2,1,0:T(8,128)S(1)}, f32[1,56,2560]{2,1,0:T(8,128)S(1)}, u32[]{:S(2)}, u32[]{:S(2)}) collective-permute-start(f32[1,56,2560]{2,1,0:T(8,128)S(1)} %broadcast_select_fusion.28), channel_id=16, source_target_pairs={{0,1},{1,2},{2,3},{3,4},{4,5},{5,6},{6,7},{7,8},{8,9},{9,10},{10,1... | collective-permute-start | bytes 1720328 | tf_op jit(solution)/vmap(transpose(jvp()))/dot_general | solution.py:21
  778.8 18.8 %collective-permute-start.9 = (f32[1,56,2560]{2,1,0:T(8,128)S(1)}, f32[1,56,2560]{2,1,0:T(8,128)S(1)}, u32[]{:S(2)}, u32[]{:S(2)}) collective-permute-start(f32[1,56,2560]{2,1,0:T(8,128)S(1)} %broadcast_select_fusion.29), channel_id=15, source_target_pairs={{0,15},{1,0},{2,1},{3,2},{4,3},{5,4},{6,5},{7,6},{8,7},{9,8},{10,9... | collective-permute-start | bytes 1720328 | tf_op jit(solution)/vmap(transpose(jvp()))/dot_general | solution.py:21
  797.8 17.5 %collective-permute-start.10 = (f32[1,56,2560]{2,1,0:T(8,128)S(1)}, f32[1,56,2560]{2,1,0:T(8,128)S(1)}, u32[]{:S(2)}, u32[]{:S(2)}) collective-permute-start(f32[1,56,2560]{2,1,0:T(8,128)S(1)} %get-tuple-element.474), channel_id=18, source_target_pairs={{0,1},{1,2},{2,3},{3,4},{4,5},{5,6},{6,7},{7,8},{8,9},{9,10},{10,1... | collective-permute-start | bytes 1720328 | tf_op jit(solution)/vmap(transpose(jvp()))/dot_general | solution.py:21
  862.6 466.4 %all-gather.14.cloned.1.call-start = ((), (), s32[]{:S(2)}) async-start(), calls=%async_computation.2 | async-start | bytes 9748480 | tf_op jit(solution)/reshape | solution.py:52
  883.3 27.3 %collective-permute-start.20 = (f32[1,160,896]{2,1,0:T(8,128)S(1)}, f32[1,160,896]{2,1,0:T(8,128)S(1)}, u32[]{:S(2)}, u32[]{:S(2)}) collective-permute-start(f32[1,160,896]{2,1,0:T(8,128)S(1)} %broadcast_select_fusion.34), channel_id=35, source_target_pairs={{0,1},{1,2},{2,3},{3,4},{4,5},{5,6},{6,7},{7,8},{8,9},{9,10},{10,1... | collective-permute-start | bytes 1720328 | tf_op jit(solution)/vmap(transpose(jvp()))/dot_general | solution.py:9
  883.4 27.2 %collective-permute-start.21 = (f32[1,160,896]{2,1,0:T(8,128)S(1)}, f32[1,160,896]{2,1,0:T(8,128)S(1)}, u32[]{:S(2)}, u32[]{:S(2)}) collective-permute-start(f32[1,160,896]{2,1,0:T(8,128)S(1)} %broadcast_select_fusion.35), channel_id=34, source_target_pairs={{0,15},{1,0},{2,1},{3,2},{4,3},{5,4},{6,5},{7,6},{8,7},{9,8},{10,9... | collective-permute-start | bytes 1720328 | tf_op jit(solution)/vmap(transpose(jvp()))/dot_general | solution.py:9
  910.7 22.8 %collective-permute-start.22 = (f32[1,160,896]{2,1,0:T(8,128)S(1)}, f32[1,160,896]{2,1,0:T(8,128)S(1)}, u32[]{:S(2)}, u32[]{:S(2)}) collective-permute-start(f32[1,160,896]{2,1,0:T(8,128)S(1)} %get-tuple-element.501), channel_id=37, source_target_pairs={{0,1},{1,2},{2,3},{3,4},{4,5},{5,6},{6,7},{7,8},{8,9},{9,10},{10,1... | collective-permute-start | bytes 1720328 | tf_op jit(solution)/vmap(transpose(jvp()))/dot_general | solution.py:9
  913.3 22.6 %collective-permute-start.23 = (f32[1,160,896]{2,1,0:T(8,128)S(1)}, f32[1,160,896]{2,1,0:T(8,128)S(1)}, u32[]{:S(2)}, u32[]{:S(2)}) collective-permute-start(f32[1,160,896]{2,1,0:T(8,128)S(1)} %get-tuple-element.502), channel_id=36, source_target_pairs={{0,15},{1,0},{2,1},{3,2},{4,3},{5,4},{6,5},{7,6},{8,7},{9,8},{10,9... | collective-permute-start | bytes 1720328 | tf_op jit(solution)/vmap(transpose(jvp()))/dot_general | solution.py:9
  938.0 30.2 %collective-permute-start.20 = (f32[1,160,896]{2,1,0:T(8,128)S(1)}, f32[1,160,896]{2,1,0:T(8,128)S(1)}, u32[]{:S(2)}, u32[]{:S(2)}) collective-permute-start(f32[1,160,896]{2,1,0:T(8,128)S(1)} %broadcast_select_fusion.34), channel_id=35, source_target_pairs={{0,1},{1,2},{2,3},{3,4},{4,5},{5,6},{6,7},{7,8},{8,9},{9,10},{10,1... | collective-permute-start | bytes 1720328 | tf_op jit(solution)/vmap(transpose(jvp()))/dot_general | solution.py:9
  957.0 18.9 %collective-permute-start.21 = (f32[1,160,896]{2,1,0:T(8,128)S(1)}, f32[1,160,896]{2,1,0:T(8,128)S(1)}, u32[]{:S(2)}, u32[]{:S(2)}) collective-permute-start(f32[1,160,896]{2,1,0:T(8,128)S(1)} %broadcast_select_fusion.35), channel_id=34, source_target_pairs={{0,15},{1,0},{2,1},{3,2},{4,3},{5,4},{6,5},{7,6},{8,7},{9,8},{10,9... | collective-permute-start | bytes 1720328 | tf_op jit(solution)/vmap(transpose(jvp()))/dot_general | solution.py:9
  976.0 17.5 %collective-permute-start.22 = (f32[1,160,896]{2,1,0:T(8,128)S(1)}, f32[1,160,896]{2,1,0:T(8,128)S(1)}, u32[]{:S(2)}, u32[]{:S(2)}) collective-permute-start(f32[1,160,896]{2,1,0:T(8,128)S(1)} %get-tuple-element.501), channel_id=37, source_target_pairs={{0,1},{1,2},{2,3},{3,4},{4,5},{5,6},{6,7},{7,8},{8,9},{9,10},{10,1... | collective-permute-start | bytes 1720328 | tf_op jit(solution)/vmap(transpose(jvp()))/dot_general | solution.py:9
  999.3 17.4 %collective-permute-start.20 = (f32[1,160,896]{2,1,0:T(8,128)S(1)}, f32[1,160,896]{2,1,0:T(8,128)S(1)}, u32[]{:S(2)}, u32[]{:S(2)}) collective-permute-start(f32[1,160,896]{2,1,0:T(8,128)S(1)} %broadcast_select_fusion.34), channel_id=35, source_target_pairs={{0,1},{1,2},{2,3},{3,4},{4,5},{5,6},{6,7},{7,8},{8,9},{9,10},{10,1... | collective-permute-start | bytes 1720328 | tf_op jit(solution)/vmap(transpose(jvp()))/dot_general | solution.py:9
  1052.1 17.5 %collective-permute-start.22 = (f32[1,160,896]{2,1,0:T(8,128)S(1)}, f32[1,160,896]{2,1,0:T(8,128)S(1)}, u32[]{:S(2)}, u32[]{:S(2)}) collective-permute-start(f32[1,160,896]{2,1,0:T(8,128)S(1)} %get-tuple-element.501), channel_id=37, source_target_pairs={{0,1},{1,2},{2,3},{3,4},{4,5},{5,6},{6,7},{7,8},{8,9},{9,10},{10,1... | collective-permute-start | bytes 1720328 | tf_op jit(solution)/vmap(transpose(jvp()))/dot_general | solution.py:9
  1052.1 17.5 %collective-permute-start.23 = (f32[1,160,896]{2,1,0:T(8,128)S(1)}, f32[1,160,896]{2,1,0:T(8,128)S(1)}, u32[]{:S(2)}, u32[]{:S(2)}) collective-permute-start(f32[1,160,896]{2,1,0:T(8,128)S(1)} %get-tuple-element.502), channel_id=36, source_target_pairs={{0,15},{1,0},{2,1},{3,2},{4,3},{5,4},{6,5},{7,6},{8,7},{9,8},{10,9... | collective-permute-start | bytes 1720328 | tf_op jit(solution)/vmap(transpose(jvp()))/dot_general | solution.py:9
  1070.5 167.3 %collective-permute-start.29 = (f32[1,160,896]{2,1,0:T(8,128)}, f32[1,160,896]{2,1,0:T(8,128)}, u32[]{:S(2)}, u32[]{:S(2)}) collective-permute-start(f32[1,160,896]{2,1,0:T(8,128)} %get-tuple-element.47), channel_id=38, source_target_pairs={{0,1},{1,2},{2,3},{3,4},{4,5},{5,6},{6,7},{7,8},{8,9},{9,10},{10,1... | collective-permute-start | bytes 1720328 | tf_op jit(solution)/vmap(transpose(jvp()))/dot_general | solution.py:9
  1108.1 17.5 %collective-permute-start.18 = (f32[1,160,896]{2,1,0:T(8,128)S(1)}, f32[1,160,896]{2,1,0:T(8,128)S(1)}, u32[]{:S(2)}, u32[]{:S(2)}) collective-permute-start(f32[1,160,896]{2,1,0:T(8,128)S(1)} %get-tuple-element.492), channel_id=31, source_target_pairs={{0,1},{1,2},{2,3},{3,4},{4,5},{5,6},{6,7},{7,8},{8,9},{9,10},{10,1... | collective-permute-start | bytes 1720328 | tf_op jit(solution)/vmap(transpose(jvp()))/dot_general | solution.py:9
  1108.1 17.5 %collective-permute-start.19 = (f32[1,160,896]{2,1,0:T(8,128)S(1)}, f32[1,160,896]{2,1,0:T(8,128)S(1)}, u32[]{:S(2)}, u32[]{:S(2)}) collective-permute-start(f32[1,160,896]{2,1,0:T(8,128)S(1)} %get-tuple-element.493), channel_id=30, source_target_pairs={{0,15},{1,0},{2,1},{3,2},{4,3},{5,4},{6,5},{7,6},{8,7},{9,8},{10,9... | collective-permute-start | bytes 1720328 | tf_op jit(solution)/vmap(transpose(jvp()))/dot_general | solution.py:9
  1127.7 17.6 %collective-permute-start.16 = (f32[1,160,896]{2,1,0:T(8,128)S(1)}, f32[1,160,896]{2,1,0:T(8,128)S(1)}, u32[]{:S(2)}, u32[]{:S(2)}) collective-permute-start(f32[1,160,896]{2,1,0:T(8,128)S(1)} %broadcast_select_fusion.32), channel_id=29, source_target_pairs={{0,1},{1,2},{2,3},{3,4},{4,5},{5,6},{6,7},{7,8},{8,9},{9,10},{10,1... | collective-permute-start | bytes 1720328 | tf_op jit(solution)/vmap(transpose(jvp()))/dot_general | solution.py:9
  1127.8 17.5 %collective-permute-start.17 = (f32[1,160,896]{2,1,0:T(8,128)S(1)}, f32[1,160,896]{2,1,0:T(8,128)S(1)}, u32[]{:S(2)}, u32[]{:S(2)}) collective-permute-start(f32[1,160,896]{2,1,0:T(8,128)S(1)} %broadcast_select_fusion.33), channel_id=28, source_target_pairs={{0,15},{1,0},{2,1},{3,2},{4,3},{5,4},{6,5},{7,6},{8,7},{9,8},{10,9... | collective-permute-start | bytes 1720328 | tf_op jit(solution)/vmap(transpose(jvp()))/dot_general | solution.py:9
  1145.4 17.7 %collective-permute-start.18 = (f32[1,160,896]{2,1,0:T(8,128)S(1)}, f32[1,160,896]{2,1,0:T(8,128)S(1)}, u32[]{:S(2)}, u32[]{:S(2)}) collective-permute-start(f32[1,160,896]{2,1,0:T(8,128)S(1)} %get-tuple-element.492), channel_id=31, source_target_pairs={{0,1},{1,2},{2,3},{3,4},{4,5},{5,6},{6,7},{7,8},{8,9},{9,10},{10,1... | collective-permute-start | bytes 1720328 | tf_op jit(solution)/vmap(transpose(jvp()))/dot_general | solution.py:9
  1145.5 17.7 %collective-permute-start.19 = (f32[1,160,896]{2,1,0:T(8,128)S(1)}, f32[1,160,896]{2,1,0:T(8,128)S(1)}, u32[]{:S(2)}, u32[]{:S(2)}) collective-permute-start(f32[1,160,896]{2,1,0:T(8,128)S(1)} %get-tuple-element.493), channel_id=30, source_target_pairs={{0,15},{1,0},{2,1},{3,2},{4,3},{5,4},{6,5},{7,6},{8,7},{9,8},{10,9... | collective-permute-start | bytes 1720328 | tf_op jit(solution)/vmap(transpose(jvp()))/dot_general | solution.py:9
  1182.3 17.6 %collective-permute-start.18 = (f32[1,160,896]{2,1,0:T(8,128)S(1)}, f32[1,160,896]{2,1,0:T(8,128)S(1)}, u32[]{:S(2)}, u32[]{:S(2)}) collective-permute-start(f32[1,160,896]{2,1,0:T(8,128)S(1)} %get-tuple-element.492), channel_id=31, source_target_pairs={{0,1},{1,2},{2,3},{3,4},{4,5},{5,6},{6,7},{7,8},{8,9},{9,10},{10,1... | collective-permute-start | bytes 1720328 | tf_op jit(solution)/vmap(transpose(jvp()))/dot_general | solution.py:9
  1182.3 17.5 %collective-permute-start.19 = (f32[1,160,896]{2,1,0:T(8,128)S(1)}, f32[1,160,896]{2,1,0:T(8,128)S(1)}, u32[]{:S(2)}, u32[]{:S(2)}) collective-permute-start(f32[1,160,896]{2,1,0:T(8,128)S(1)} %get-tuple-element.493), channel_id=30, source_target_pairs={{0,15},{1,0},{2,1},{3,2},{4,3},{5,4},{6,5},{7,6},{8,7},{9,8},{10,9... | collective-permute-start | bytes 1720328 | tf_op jit(solution)/vmap(transpose(jvp()))/dot_general | solution.py:9
  1219.1 17.7 %collective-permute-start.18 = (f32[1,160,896]{2,1,0:T(8,128)S(1)}, f32[1,160,896]{2,1,0:T(8,128)S(1)}, u32[]{:S(2)}, u32[]{:S(2)}) collective-permute-start(f32[1,160,896]{2,1,0:T(8,128)S(1)} %get-tuple-element.492), channel_id=31, source_target_pairs={{0,1},{1,2},{2,3},{3,4},{4,5},{5,6},{6,7},{7,8},{8,9},{9,10},{10,1... | collective-permute-start | bytes 1720328 | tf_op jit(solution)/vmap(transpose(jvp()))/dot_general | solution.py:9
  1219.2 17.7 %collective-permute-start.19 = (f32[1,160,896]{2,1,0:T(8,128)S(1)}, f32[1,160,896]{2,1,0:T(8,128)S(1)}, u32[]{:S(2)}, u32[]{:S(2)}) collective-permute-start(f32[1,160,896]{2,1,0:T(8,128)S(1)} %get-tuple-element.493), channel_id=30, source_target_pairs={{0,15},{1,0},{2,1},{3,2},{4,3},{5,4},{6,5},{7,6},{8,7},{9,8},{10,9... | collective-permute-start | bytes 1720328 | tf_op jit(solution)/vmap(transpose(jvp()))/dot_general | solution.py:9
  (101 other events, 1593.5 us)
Sparse Core Ops, SparseCore 0:
  659.9 137.0 all-gather.9
  862.7 115.1 all-gather.11
  1253.8 75.1 all-gather.13
where the time goes:
time: 1370 us; the launch traced here: 1360 us
  waiting for transfers between devices  488 us (36%)
  matrix products  378 us (28%)
  starting transfers between devices  262 us (19%)
  local copies, waits for them, and re-layouts  92.5 us (7%)
  other arithmetic  75.3 us (5%)
  loops' own time  48.6 us (4%)
  between operations  15.1 us (1%)
    dot_general x34, waiting for transfers between devices, matmul(): jnp.dot(a, w, preferred_element_type=jnp.float32).astype(jnp.bfloat16)  153 us
    dot_general x34, waiting for transfers between devices, layer(): up = jnp.dot(a, w['w_up'], preferred_element_type=jnp.float32)  152 us
    dot_general x19, matrix products, matmul(): jnp.dot(a, w, preferred_element_type=jnp.float32).astype(jnp.bfloat16)  136 us
    dot_general x19, matrix products, layer(): up = jnp.dot(a, w['w_up'], preferred_element_type=jnp.float32)  125 us
    dot_general x19, matrix products, layer(): gate = jnp.dot(a, w['w_gate'], preferred_element_type=jnp.float32)  116 us
    dot_general x34, waiting for transfers between devices, layer(): gate = jnp.dot(a, w['w_gate'], preferred_element_type=jnp.float32)  108 us
    dot_general x34, starting transfers between devices, layer(): up = jnp.dot(a, w['w_up'], preferred_element_type=jnp.float32)  96.5 us
    dot_general x34, starting transfers between devices, matmul(): jnp.dot(a, w, preferred_element_type=jnp.float32).astype(jnp.bfloat16)  91.7 us
  transfers between devices with their start and end apart: 105, of which 62 were waited for; matrix products, arithmetic and copies ran while one was open for 22% of the time, Pallas kernels for 0%

commit v1 on v0

v1 whole, which is shorter than its diff:
```python
import functools

import jax
import jax.numpy as jnp
from jax import lax
from jax.experimental import pallas as pl
from jax.experimental.pallas import tpu as pltpu
from jax.sharding import PartitionSpec as P

F32, BF16 = jnp.float32, jnp.bfloat16


def dot(a, b, contract):
    return lax.dot_general(a, b, (contract, ((), ())), preferred_element_type=F32)


def nn(a, b):
    return dot(a, b, ((1,), (0,)))


def nt(a, b):
    return dot(a, b, ((1,), (1,)))


def tn(a, b):
    return dot(a, b, ((0,), (0,)))


def adamw(w, m, v, g):
    m = 0.9 * m + 0.1 * g
    v = 0.95 * v + 0.05 * g * g
    step = m * lax.rsqrt(v + 1e-8) + 0.1 * w
    return (w - 0.02 * step).astype(BF16), m, v


def normed(h):
    wide = h.astype(F32)
    scale = lax.rsqrt(jnp.mean(wide**2, -1, keepdims=True) + 1e-6)
    return (wide * scale).astype(BF16)


def normed_back(h, da):
    wide, da = h.astype(F32), da.astype(F32)
    scale = lax.rsqrt(jnp.mean(wide**2, -1, keepdims=True) + 1e-6)
    inner = jnp.mean(wide * da, -1, keepdims=True)
    return (da * scale - wide * (scale * scale * scale * inner)).astype(BF16)


def hidden(a, wg, wu):
    gate, up = nn(a, wg), nn(a, wu)
    return gate, up, (jax.nn.silu(gate) * up).astype(BF16)


def hidden_back(gate, up, dact):
    s = jax.nn.sigmoid(gate)
    dact = dact.astype(F32)
    dup = dact * gate * s
    dgate = dact * up * (s * (1.0 + gate * (1.0 - s)))
    return dgate.astype(BF16), dup.astype(BF16)


MESH = pl.DeviceIdType.MESH


def ring_kernel(order, shapes, *refs):
    n = len(order)
    take = iter(refs)
    g = [next(take) for _ in range(n)]
    w, m, v = ([next(take) for _ in range(3)] for _ in range(3))
    w_new, m_new, v_new = ([next(take) for _ in range(3)] for _ in range(3))
    own, sib, rec, wv, mv, vv = ([next(take) for _ in range(n)] for _ in range(6))
    (own_sem, sib_send, sib_recv, rs_send, rs_recv, ag_send, ag_recv, pass_send, pass_recv, load_sem, store_sem) = take

    me = lax.axis_index("dp")
    core, chip = me % 2, me // 2
    far = chip // 4
    place = chip * (1 - far) + far * (11 - chip)
    way = 1 - 2 * core

    def chip_at(p):
        p = (p + 16) % 8
        half = p // 4
        return p * (1 - half) + half * (11 - p)

    after = 2 * chip_at(place + way) + core
    before = 2 * chip_at(place - way) + core
    twin = me + way

    barrier = pltpu.get_barrier_semaphore()
    for other in (after, before, twin):
        pl.semaphore_signal(barrier, inc=1, device_id={"dp": other}, device_id_type=MESH)

    def own_copy(k, j):
        t = chip_at(place - way * (1 + j))
        return pltpu.make_async_copy(g[k].at[t, core], own[k].at[j], own_sem.at[k, j])

    def sib_copy(k, j):
        t = chip_at(place + way * (1 + j))
        return pltpu.make_async_remote_copy(
            g[k].at[t, 1 - core], sib[k].at[j], sib_send.at[k, j], sib_recv.at[k, j], {"dp": twin}, MESH
        )

    def ring_copy(k, j):
        return pltpu.make_async_remote_copy(
            own[k].at[j], rec[k].at[j], rs_send.at[k, j], rs_recv.at[k, j], {"dp": after}, MESH
        )

    def loads(k):
        name, layer = order[k]
        return (
            pltpu.make_async_copy(w[name].at[layer, me], wv[k], load_sem.at[k, 0]),
            pltpu.make_async_copy(m[name].at[layer], mv[k], load_sem.at[k, 1]),
            pltpu.make_async_copy(v[name].at[layer], vv[k], load_sem.at[k, 2]),
        )

    def stores(k):
        name, layer = order[k]
        return (
            pltpu.make_async_copy(wv[k], w_new[name].at[layer, me], store_sem.at[k, 0]),
            pltpu.make_async_copy(mv[k], m_new[name].at[layer], store_sem.at[k, 1]),
            pltpu.make_async_copy(vv[k], v_new[name].at[layer], store_sem.at[k, 2]),
        )

    def gather_copy(k, j, source):
        name, layer = order[k]
        at = 2 * chip_at(place - way * j) + core
        there = w_new[name].at[layer, at]
        source = there if source is None else source
        return pltpu.make_async_remote_copy(source, there, ag_send.at[k, j], ag_recv.at[k, j], {"dp": after}, MESH)

    def twin_copy(k, j, source):
        name, layer = order[k]
        at = 2 * chip_at(place - way * j) + core
        there = w_new[name].at[layer, at]
        source = there if source is None else source
        return pltpu.make_async_remote_copy(source, there, pass_send.at[k, j], pass_recv.at[k, j], {"dp": twin}, MESH)

    def over_columns(k, body):
        rows, columns = shapes[order[k][0]]
        wide = 256 if columns % 256 == 0 and rows < 100 else 128

        def piece(c, carry):
            body(pl.ds(pl.multiple_of(c * wide, wide), wide))
            return carry

        lax.fori_loop(0, columns // wide, piece, 0)

    @pl.loop(0, 8)
    def _(j):
        for k in range(n):
            own_copy(k, j).start()

    pl.semaphore_wait(barrier, 3)

    @pl.loop(0, 8)
    def _(j):
        for k in range(n):
            sib_copy(k, j).start()

    for k in range(n):
        for copy in loads(k):
            copy.start()

    def first(k):
        own_copy(k, 0).wait()
        sib_copy(k, 0).wait_recv()

        def add(at):
            own[k][0, :, at] = (own[k][0, :, at].astype(F32) + sib[k][0, :, at].astype(F32)).astype(BF16)

        over_columns(k, add)
        ring_copy(k, 0).start()

    for k in range(n):
        first(k)

    @pl.loop(1, 7)
    def _(j):
        for k in range(n):
            own_copy(k, j).wait()
            sib_copy(k, j).wait_recv()
            ring_copy(k, j - 1).wait_recv()

            def add(at, k=k):
                total = own[k][j, :, at].astype(F32) + sib[k][j, :, at].astype(F32) + rec[k][j - 1, :, at].astype(F32)
                own[k][j, :, at] = total.astype(BF16)

            over_columns(k, add)
            ring_copy(k, j).start()

    for k in range(n):
        own_copy(k, 7).wait()
        sib_copy(k, 7).wait_recv()
        ring_copy(k, 6).wait_recv()
        for copy in loads(k):
            copy.wait()

        def step(at, k=k):
            total = own[k][7, :, at].astype(F32) + sib[k][7, :, at].astype(F32) + rec[k][6, :, at].astype(F32)
            w_at, m_at, v_at = adamw(wv[k][:, at].astype(F32), mv[k][:, at], vv[k][:, at], total.astype(BF16).astype(F32))
            wv[k][:, at] = w_at
            mv[k][:, at] = m_at
            vv[k][:, at] = v_at

        over_columns(k, step)
        gather_copy(k, 0, wv[k]).start()
        twin_copy(k, 0, wv[k]).start()
        for copy in stores(k):
            copy.start()

    @pl.loop(1, 7)
    def _(j):
        for k in range(n):
            gather_copy(k, j - 1, None).wait_recv()
            gather_copy(k, j, None).start()
            twin_copy(k, j, None).start()

    for k in range(n):
        gather_copy(k, 6, None).wait_recv()
        twin_copy(k, 7, None).start()

    @pl.loop(0, 8)
    def _(j):
        for k in range(n):
            sib_copy(k, j).wait_send()
            twin_copy(k, j, None).wait()

    @pl.loop(0, 7)
    def _(j):
        for k in range(n):
            ring_copy(k, j).wait_send()
            gather_copy(k, j, None).wait_send()

    for k in range(n):
        for copy in stores(k):
            copy.wait()


ORDER = ((2, 1), (0, 1), (1, 1), (2, 0), (0, 0), (1, 0))


def ring_step(grads, w, m, v):
    n, shapes = len(ORDER), [one.shape[1:] for one in m]
    dma = pltpu.SemaphoreType.DMA
    scratch = [pltpu.VMEM((blocks, *shapes[name]), BF16) for blocks in (8, 8, 7) for name, _ in ORDER]
    scratch += [pltpu.VMEM(shapes[name], dtype) for dtype in (BF16, F32, F32) for name, _ in ORDER]
    scratch += [dma((n, 8))] * 3 + [dma((n, 7))] * 4 + [dma((n, 8))] * 2 + [dma((n, 3))] * 2
    anywhere = pl.BlockSpec(memory_space=pl.ANY)
    return pl.pallas_call(
        functools.partial(ring_kernel, ORDER, shapes),
        out_shape=[jax.ShapeDtypeStruct(one.shape, one.dtype) for one in (*w, *m, *v)],
        in_specs=[anywhere] * (n + 9),
        out_specs=[anywhere] * 9,
        scratch_shapes=scratch,
        compiler_params=pltpu.CompilerParams(collective_id=0, has_side_effects=True, vmem_limit_bytes=67_000_000),
        name="ring_step",
    )(*grads, *w, *m, *v)


def solution(mesh):
    def body(x, dy, wg, wu, wd, mg, mu, md, vg, vu, vd):
        x, dy = x[0], dy[0]
        a0 = normed(x)
        gate0, up0, act0 = hidden(a0, wg[0], wu[0])
        h1 = x + nn(act0, wd[0]).astype(BF16)
        a1 = normed(h1)
        gate1, up1, act1 = hidden(a1, wg[1], wu[1])
        dact1 = nt(dy, wd[1]).astype(BF16)
        dwd1 = tn(act1, dy).astype(BF16)
        dgate1, dup1 = hidden_back(gate1, up1, dact1)
        dwg1, dwu1 = tn(a1, dgate1).astype(BF16), tn(a1, dup1).astype(BF16)
        da1 = nt(dgate1, wg[1]).astype(BF16) + nt(dup1, wu[1]).astype(BF16)
        dh1 = dy + normed_back(h1, da1)
        dact0 = nt(dh1, wd[0]).astype(BF16)
        dwd0 = tn(act0, dh1).astype(BF16)
        dgate0, dup0 = hidden_back(gate0, up0, dact0)
        dwg0, dwu0 = tn(a0, dgate0).astype(BF16), tn(a0, dup0).astype(BF16)

        def blocks(one):
            return one.reshape(2, 16, -1, one.shape[-1])

        def by_chip(one):
            return one.reshape(8, 2, -1, one.shape[-1])

        grads = [by_chip(one) for one in (dwd1, dwg1, dwu1, dwd0, dwg0, dwu0)]
        new = ring_step(grads, [blocks(one) for one in (wg, wu, wd)], [mg, mu, md], [vg, vu, vd])
        return tuple(one.reshape(2, -1, one.shape[-1]) for one in new[:3]) + tuple(new[3:])

    one, shard = P(("rep", "dp"), None, None), P(None, "dp", None)
    rep = P(None, None, None)
    outs = (P("rep", None, None),) * 3 + (P("rep", "dp", None),) * 6
    return jax.shard_map(body, mesh=mesh, in_specs=(one, one, rep, rep, rep) + (shard,) * 6, out_specs=outs, check_vma=False)
```

time: 1370 us -> 608 us (0.44)
  waiting for transfers between devices: 488 us -> 0 us
  Pallas kernels: 0 us -> 271 us
  starting transfers between devices: 262 us -> 0 us
  matrix products: 378 us -> 277 us
  other arithmetic: 75.3 us -> 9.84 us
  local copies, waits for them, and re-layouts: 92.5 us -> 42.2 us
  loops' own time: 48.6 us -> 0 us
  between operations: 15.1 us -> 1.35 us
    dot_general x102 -> x0, waiting for transfers between devices: 413 us -> none  [the longest x34 153 us: matmul(): jnp.dot(a, w, preferred_element_type=jnp.float32).astype(jnp.bfloat16)]
    pallas_call x0 -> x1, Pallas kernels: none -> 271 us  [ring_step(): pl.pallas_call(functools.partial(ring_kernel, ORDER, shapes), out_shape=[...]
    dot_general x102 -> x0, starting transfers between devices: 262 us -> none  [the longest x34 96.5 us: layer(): up = jnp.dot(a, w['w_up'], preferred_element_type=jnp.float32)]
    dot_general x57 -> x15, matrix products: 378 us -> 277 us  [dot(): lax.dot_general(a, b, (contract, ((), ())), preferred_element_type=F32)]
    reshape x3 -> x0, waiting for transfers between devices: 75.3 us -> none  [step(): t.reshape(-1, *t.shape[2:])]
    another operation x6 -> x0, loops' own time: 48.6 us -> none  [the longest x2 16.3 us: layer(): gate = jnp.dot(a, w['w_gate'], preferred_element_type=jnp.float32)]
    dot_general x96 -> x0, other arithmetic: 41 us -> none
    unnamed x33 -> x63, local copies, waits for them, and re-layouts: 77.7 us -> 42.2 us
  transfers between devices with their start and end apart: 105 -> 0, of which waited for: 62 -> 0; matrix products, arithmetic and copies ran while one was open for 22% -> 0% of each run, Pallas kernels for 0% -> 0%
where the time goes in v1:
time: 608 us; the launch traced here: 601 us
  matrix products  277 us (46%)
  Pallas kernels  271 us (45%)
  local copies, waits for them, and re-layouts  42.2 us (7%)
  other arithmetic  9.84 us (2%)
    dot_general x15, matrix products, dot(): lax.dot_general(a, b, (contract, ((), ())), preferred_element_type=F32)  277 us
    pallas_call x1, Pallas kernels, ring_step(): pl.pallas_call(functools.partial(ring_kernel, ORDER, shapes), out_shape=[...  271 us
    unnamed x63, local copies, waits for them, and re-layouts  42.2 us

profile of v1, /device:TPU:0, one launch (start us, length us, event | category | flops | bytes accessed | tf_op | source)
XLA Modules:
  0.0 600.8 jit_solution(15024452077932204902)
XLA Ops:
  0.6 6.1 %copy.20 = bf16[1,2048,896]{1,2,0:T(8,128)(2,1)} copy(bf16[1,2048,896]{2,1,0:T(8,128)(2,1)} %param.11) | data formatting | bytes 7340032 | tf_op args[0]
  6.8 2.8 fusion.13
  9.6 0.0 copy-start.1
  9.6 18.3 %fusion.41 = f32[2048,2560]{1,0:T(8,128)} fusion(bf16[2,896,2560]{2,1,0:T(8,128)(2,1)} %param.13, bf16[1,2048,896]{2,1,0:T(8,128)(2,1)} %param.11, f32[2048]{0:T(1024)S(1)} %add_rsqrt_fusion.1), kind=kOutput, calls=%fused_computation.56 | convolution fusion | flops 9400745984 | bytes 29237248 | tf_op jit(solution)/shard_map/dot_general | solution.py:14
  27.9 0.0 copy-done.1
  27.9 24.5 %multiply_convert_fusion.1 = (bf16[2048,2560]{1,0:T(8,128)(2,1)}, f32[2048,2560]{1,0:T(8,128)}) fusion(f32[2048,2560]{1,0:T(8,128)} %fusion.41, bf16[2,896,2560]{2,1,0:T(8,128)(2,1)} %param.14, bf16[1,2048,896]{2,1,0:T(8,128)(2,1)S(1)} %copy-done.1, f32[2048]{0:T(1024)S(1)} %add_rsqrt_fusion.1), kind=kOutput, calls=%fused_computation.14 | convolution fusion | flops 9432203264 | bytes 60694528 | tf_op jit(solution)/shard_map/dot_general | solution.py:14
  52.4 0.0 copy-done
  52.4 15.9 %fusion.17 = (f32[2048]{0:T(1024)S(1)}, bf16[2048,896]{0,1:T(8,128)(2,1)}) fusion(bf16[2048,2560]{1,0:T(8,128)(2,1)} %get-tuple-element.29, bf16[2,2560,896]{2,1,0:T(8,128)(2,1)} %param.15, bf16[1,2048,896]{1,2,0:T(8,128)(2,1)S(1)} %copy-done), kind=kOutput, calls=%fused_computation.32 | convolution fusion | flops 9404413952 | bytes 22421504 | tf_op jit(solution)/shard_map/dot_general | solution.py:14
  68.3 0.0 copy-start.2
  68.3 0.0 slice-start.3
  68.4 0.0 slice-start.4
  68.4 18.4 %fusion.30 = f32[2048,2560]{1,0:T(8,128)} fusion(bf16[2,896,2560]{2,1,0:T(8,128)(2,1)} %param.14, bf16[2048,896]{0,1:T(8,128)(2,1)} %get-tuple-element.32, f32[2048]{0:T(1024)S(1)} %add_rsqrt_fusion), kind=kOutput, calls=%fused_computation.45 | convolution fusion | flops 9400745984 | bytes 29237248 | tf_op jit(solution)/shard_map/dot_general | solution.py:14
  86.8 16.0 %convolution_convert_fusion.1 = bf16[2048,2560]{1,0:T(8,128)(2,1)} fusion(bf16[2,2560,896]{2,1,0:T(8,128)(2,1)} %param.15, bf16[1,2048,896]{2,1,0:T(8,128)(2,1)S(1)} %copy-done.2), kind=kOutput, calls=%fused_computation.21 | convolution fusion | flops 9400483840 | bytes 18743296 | tf_op jit(solution)/shard_map/dot_general | solution.py:14
  102.7 0.0 slice-done.4
  102.7 32.7 %fusion.3 = (bf16[2048,2560]{1,0:T(8,128)(2,1)}, bf16[2048,2560]{1,0:T(8,128)(2,1)}, f32[2048,2560]{1,0:T(8,128)}) fusion(bf16[2048,2560]{1,0:T(8,128)(2,1)} %convolution_convert_fusion.1, f32[2048,2560]{1,0:T(8,128)} %fusion.30, bf16[2,896,2560]{2,1,0:T(8,128)(2,1)S(1)} %bitcast.84, bf16[2048,896]{0,1:T(8,128)(2,1)} %get-tuple-element.32, ...), kind=kOutput, calls=%fused_computation.7 | convolution fusion | flops 9474146304 | bytes 81666048 | tf_op jit(solution)/shard_map/dot_general | solution.py:14
  135.4 21.9 %fusion.26 = bf16[2560,896]{1,0:T(8,128)(2,1)} fusion(f32[2048,2560]{1,0:T(8,128)} %fusion.30, f32[2048,2560]{1,0:T(8,128)} %get-tuple-element.33, bf16[1,2048,896]{2,1,0:T(8,128)(2,1)} %param.12), kind=kOutput, calls=%fused_computation.38 | convolution fusion | flops 9428992000 | bytes 50200576 | tf_op jit(solution)/shard_map/dot_general | solution.py:14
  157.4 15.0 %convolution_convert_fusion.4 = bf16[896,2560]{1,0:T(8,128)(2,1)} fusion(bf16[2048,2560]{1,0:T(8,128)(2,1)} %get-tuple-element.28, bf16[2048,896]{0,1:T(8,128)(2,1)} %get-tuple-element.32, f32[2048]{0:T(1024)S(1)} %add_rsqrt_fusion), kind=kOutput, calls=%fused_computation.41 | convolution fusion | flops 9403039744 | bytes 18751488 | tf_op jit(solution)/shard_map/dot_general | solution.py:14
  172.3 0.0 copy-done.3
  172.4 0.0 slice-start.7
  172.4 14.1 %convolution_convert_fusion.3 = bf16[896,2560]{1,0:T(8,128)(2,1)} fusion(bf16[2048,2560]{1,0:T(8,128)(2,1)} %get-tuple-element.27, bf16[2048,896]{0,1:T(8,128)(2,1)S(1)} %copy-done.3, f32[2048]{0:T(1024)S(1)} %add_rsqrt_fusion), kind=kOutput, calls=%fused_computation.40 | convolution fusion | flops 9403039744 | bytes 18751488 | tf_op jit(solution)/shard_map/dot_general | solution.py:14
  186.4 0.0 slice-done.1
  186.4 0.0 slice-start.8
  186.5 13.7 %fusion.28 = bf16[2048,896]{0,1:T(8,128)(2,1)} fusion(bf16[2048,2560]{1,0:T(8,128)(2,1)} %get-tuple-element.27, bf16[2,896,2560]{2,1,0:T(8,128)(2,1)S(1)} %bitcast.81), kind=kOutput, calls=%fused_computation.43 | convolution fusion | flops 9395240960 | bytes 18743296 | tf_op jit(solution)/shard_map/dot_general | solution.py:14
  200.2 0.0 slice-done.7
  200.2 14.7 %fusion.19 = (f32[2048]{0:T(1024)S(1)}, bf16[2048,896]{0,1:T(8,128)(2,1)}) fusion(bf16[2048,896]{0,1:T(8,128)(2,1)S(1)} %copy-done.3, bf16[2048,896]{0,1:T(8,128)(2,1)} %fusion.28, bf16[2048,2560]{1,0:T(8,128)(2,1)} %get-tuple-element.28, bf16[2,896,2560]{2,1,0:T(8,128)(2,1)S(1)} %bitcast.86), kind=kOutput, calls=%fused_computation.34 | convolution fusion | flops 9406248960 | bytes 26091520 | tf_op jit(solution)/shard_map/dot_general | solution.py:14
  214.8 6.1 %copy.21 = bf16[1,2048,896]{1,2,0:T(8,128)(2,1)} copy(bf16[1,2048,896]{2,1,0:T(8,128)(2,1)} %param.12) | data formatting | bytes 7340032 | tf_op args[1]
  221.0 0.0 slice-start.9
  221.0 7.0 %fusion.53 = bf16[2048,896]{0,1:T(8,128)(2,1)S(1)} fusion(bf16[2048,896]{0,1:T(8,128)(2,1)} %get-tuple-element.32, bf16[2048,896]{0,1:T(8,128)(2,1)} %get-tuple-element.35, bf16[1,2048,896]{1,2,0:T(8,128)(2,1)} %copy.21, f32[2048]{0:T(1024)S(1)} %fusion.68, f32[2048]{0:T(1024)S(1)} %add_rsqrt_fusion), kind=kLoop, calls=%fused_computation.68 | loop fusion | flops 12845056 | bytes 14696448 | tf_op jit(solution)/shard_map/add | solution.py:273
  228.0 0.0 slice-start.10
  228.0 0.0 slice-start.11
  228.0 15.6 %convolution_convert_fusion.2 = bf16[2560,896]{1,0:T(8,128)(2,1)} fusion(bf16[2048,2560]{1,0:T(8,128)(2,1)} %get-tuple-element.29, bf16[2048,896]{0,1:T(8,128)(2,1)S(1)} %fusion.53), kind=kOutput, calls=%fused_computation.39 | convolution fusion | flops 9397534720 | bytes 18743296 | tf_op jit(solution)/shard_map/dot_general | solution.py:14
  243.7 0.0 slice-done.9
  243.7 0.0 copy-start.13
  243.7 13.4 %convolution_convert_fusion = bf16[2048,2560]{1,0:T(8,128)(2,1)} fusion(bf16[2048,896]{0,1:T(8,128)(2,1)S(1)} %fusion.53, bf16[2,2560,896]{2,1,0:T(8,128)(2,1)S(1)} %bitcast.89), kind=kOutput, calls=%fused_computation.20 | convolution fusion | flops 9400483840 | bytes 18743296 | tf_op jit(solution)/shard_map/dot_general | solution.py:14
  257.1 24.0 %fusion.20 = bf16[896,2560]{1,0:T(8,128)(2,1)} fusion(f32[2048,2560]{1,0:T(8,128)} %get-tuple-element.30, bf16[2048,2560]{1,0:T(8,128)(2,1)} %convolution_convert_fusion, f32[2048,2560]{1,0:T(8,128)} %fusion.41, bf16[1,2048,896]{1,2,0:T(8,128)(2,1)} %copy.20, f32[2048]{0:T(1024)S(1)} %copy-done.13), kind=kOutput, calls=%fused_computation.36 | convolution fusion | flops 9460711424 | bytes 60694528 | tf_op jit(solution)/shard_map/dot_general | solution.py:14
  281.2 18.6 %fusion.23 = bf16[896,2560]{1,0:T(8,128)(2,1)} fusion(f32[2048,2560]{1,0:T(8,128)} %fusion.41, bf16[2048,2560]{1,0:T(8,128)(2,1)} %convolution_convert_fusion, bf16[1,2048,896]{1,2,0:T(8,128)(2,1)} %copy.20, f32[2048]{0:T(1024)S(1)} %copy-done.13), kind=kOutput, calls=%fused_computation.37 | convolution fusion | flops 9439739904 | bytes 39723008 | tf_op jit(solution)/shard_map/dot_general | solution.py:14
  299.8 270.6 %ring_step.1 = (bf16[2,16,56,2560]{3,2,1,0:T(8,128)(2,1)}, bf16[2,16,56,2560]{3,2,1,0:T(8,128)(2,1)}, bf16[2,16,160,896]{3,2,1,0:T(8,128)(2,1)}, f32[2,56,2560]{...) custom-call(bf16[8,2,160,896]{3,2,1,0:T(8,128)(2,1)} %bitcast.90, ...), custom_call_target="tpu_custom_call" | custom-call | tf_op jit(solution)/shard_map/ring_step/pallas_call | solution.py:249
  570.4 7.9 %copy.31 = bf16[2,896,2560]{2,1,0:T(8,128)(2,1)} copy(bf16[2,896,2560]{2,1,0:T(8,128)(2,1)} %bitcast.78) | data formatting | bytes 18350080
  578.3 7.8 %copy.32 = bf16[2,896,2560]{2,1,0:T(8,128)(2,1)} copy(bf16[2,896,2560]{2,1,0:T(8,128)(2,1)} %bitcast.77) | data formatting | bytes 18350080
  586.1 8.1 %copy.33 = bf16[2,2560,896]{2,1,0:T(8,128)(2,1)} copy(bf16[2,2560,896]{2,1,0:T(8,128)(2,1)} %bitcast.76) | data formatting | bytes 18350080
  594.3 0.0 copy-done.9
  594.3 1.0 copy.34
  595.3 1.0 copy.35
  596.3 1.0 copy.36
  597.3 1.0 copy.37
  598.3 0.0 copy-done.5
  598.3 1.0 copy.38
  599.3 1.0 copy.39
  (40 shorter events, 0.1 us)
Async XLA Ops:
  9.6 18.3 %copy-start.12 = (f32[2048]{0:T(1024)}, f32[2048]{0:T(1024)S(1)}, u32[]{:S(2)}) copy-start(f32[2048]{0:T(1024)S(1)} %add_rsqrt_fusion.1) | copy-start | bytes 24580
  9.6 18.3 %copy-start.1 = (bf16[1,2048,896]{2,1,0:T(8,128)(2,1)S(1)}, bf16[1,2048,896]{2,1,0:T(8,128)(2,1)}, u32[]{:S(2)}) copy-start(bf16[1,2048,896]{2,1,0:T(8,128)(2,1)} %param.11) | copy-start | bytes 11010052
  27.9 24.5 %copy-start = (bf16[1,2048,896]{1,2,0:T(8,128)(2,1)S(1)}, bf16[1,2048,896]{1,2,0:T(8,128)(2,1)}, u32[]{:S(2)}) copy-start(bf16[1,2048,896]{1,2,0:T(8,128)(2,1)} %copy.20) | copy-start | bytes 11010052
  68.3 18.4 %copy-start.10 = (f32[2048]{0:T(1024)}, f32[2048]{0:T(1024)S(1)}, u32[]{:S(2)}) copy-start(f32[2048]{0:T(1024)S(1)} %get-tuple-element.31) | copy-start | bytes 24580
  68.3 18.4 %copy-start.2 = (bf16[1,2048,896]{2,1,0:T(8,128)(2,1)S(1)}, bf16[1,2048,896]{2,1,0:T(8,128)(2,1)}, u32[]{:S(2)}) copy-start(bf16[1,2048,896]{2,1,0:T(8,128)(2,1)} %param.12) | copy-start | bytes 11010052
  68.3 34.4 %slice-start.3 = ((s8[9175040]{0:T(1024)(128)(4,1)}), s8[4194304]{0:T(1024)(128)(4,1)S(1)}, s32[]{:S(2)}) async-start(s8[9175040]{0:T(1024)(128)(4,1)} %bitcast.83), calls=%async_computation.3 | async-start | bytes 8388608
  68.4 34.4 %slice-start.4 = ((s8[9175040]{0:T(1024)(128)(4,1)}), s8[4194304]{0:T(1024)(128)(4,1)S(1)}, s32[]{:S(2)}) async-start(s8[9175040]{0:T(1024)(128)(4,1)} %bitcast.83), calls=%async_computation.4 | async-start | bytes 8388608
  86.7 16.0 %slice-start.5 = ((s8[9175040]{0:T(1024)(128)(4,1)}), s8[786432]{0:T(1024)(128)(4,1)S(1)}, s32[]{:S(2)}) async-start(s8[9175040]{0:T(1024)(128)(4,1)} %bitcast.83), calls=%async_computation.5 | async-start | bytes 1572864
  157.4 15.0 %copy-start.3 = (bf16[2048,896]{0,1:T(8,128)(2,1)S(1)}, bf16[2048,896]{0,1:T(8,128)(2,1)}, u32[]{:S(2)}) copy-start(bf16[2048,896]{0,1:T(8,128)(2,1)} %get-tuple-element.32) | copy-start | bytes 11010052
  157.4 29.1 %slice-start = ((s8[9175040]{0:T(1024)(128)(4,1)}), s8[4194304]{0:T(1024)(128)(4,1)S(1)}, s32[]{:S(2)}) async-start(s8[9175040]{0:T(1024)(128)(4,1)} %bitcast.80), calls=%async_computation | async-start | bytes 8388608
  157.4 29.1 %slice-start.1 = ((s8[9175040]{0:T(1024)(128)(4,1)}), s8[4194304]{0:T(1024)(128)(4,1)S(1)}, s32[]{:S(2)}) async-start(s8[9175040]{0:T(1024)(128)(4,1)} %bitcast.80), calls=%async_computation.1 | async-start | bytes 8388608
  172.4 14.1 %slice-start.2 = ((s8[9175040]{0:T(1024)(128)(4,1)}), s8[786432]{0:T(1024)(128)(4,1)S(1)}, s32[]{:S(2)}) async-start(s8[9175040]{0:T(1024)(128)(4,1)} %bitcast.80), calls=%async_computation.2 | async-start | bytes 1572864
  172.4 27.8 %slice-start.6 = ((s8[9175040]{0:T(1024)(128)(4,1)}), s8[4194304]{0:T(1024)(128)(4,1)S(1)}, s32[]{:S(2)}) async-start(s8[9175040]{0:T(1024)(128)(4,1)} %bitcast.85), calls=%async_computation.6 | async-start | bytes 8388608
  172.4 27.8 %slice-start.7 = ((s8[9175040]{0:T(1024)(128)(4,1)}), s8[4194304]{0:T(1024)(128)(4,1)S(1)}, s32[]{:S(2)}) async-start(s8[9175040]{0:T(1024)(128)(4,1)} %bitcast.85), calls=%async_computation.7 | async-start | bytes 8388608
  186.4 13.7 %slice-start.8 = ((s8[9175040]{0:T(1024)(128)(4,1)}), s8[786432]{0:T(1024)(128)(4,1)S(1)}, s32[]{:S(2)}) async-start(s8[9175040]{0:T(1024)(128)(4,1)} %bitcast.85), calls=%async_computation.8 | async-start | bytes 1572864
  214.8 6.1 %copy-start.11 = (f32[2048]{0:T(1024)S(1)}, f32[2048]{0:T(1024)}, u32[]{:S(2)}) copy-start(f32[2048]{0:T(1024)} %copy-done.10) | copy-start | bytes 24580
  221.0 22.7 %slice-start.9 = ((s8[9175040]{0:T(1024)(128)(4,1)}), s8[4194304]{0:T(1024)(128)(4,1)S(1)}, s32[]{:S(2)}) async-start(s8[9175040]{0:T(1024)(128)(4,1)} %bitcast.88), calls=%async_computation.9 | async-start | bytes 8388608
  228.0 15.7 %slice-start.10 = ((s8[9175040]{0:T(1024)(128)(4,1)}), s8[4194304]{0:T(1024)(128)(4,1)S(1)}, s32[]{:S(2)}) async-start(s8[9175040]{0:T(1024)(128)(4,1)} %bitcast.88), calls=%async_computation.10 | async-start | bytes 8388608
  228.0 15.7 %slice-start.11 = ((s8[9175040]{0:T(1024)(128)(4,1)}), s8[786432]{0:T(1024)(128)(4,1)S(1)}, s32[]{:S(2)}) async-start(s8[9175040]{0:T(1024)(128)(4,1)} %bitcast.88), calls=%async_computation.11 | async-start | bytes 1572864
  243.7 13.4 %copy-start.13 = (f32[2048]{0:T(1024)S(1)}, f32[2048]{0:T(1024)}, u32[]{:S(2)}) copy-start(f32[2048]{0:T(1024)} %copy-done.12) | copy-start | bytes 24580
  586.1 8.1 %copy-start.9 = (f32[2,56,2560]{2,1,0:T(8,128)S(1)}, f32[2,56,2560]{2,1,0:T(8,128)}, u32[]{:S(2)}) copy-start(f32[2,56,2560]{2,1,0:T(8,128)} %get-tuple-element.48) | copy-start | bytes 3440644
  586.1 9.2 %copy-start.8 = (f32[2,56,2560]{2,1,0:T(8,128)S(1)}, f32[2,56,2560]{2,1,0:T(8,128)}, u32[]{:S(2)}) copy-start(f32[2,56,2560]{2,1,0:T(8,128)} %get-tuple-element.49) | copy-start | bytes 3440644
  586.1 10.2 %copy-start.7 = (f32[2,160,896]{2,1,0:T(8,128)S(1)}, f32[2,160,896]{2,1,0:T(8,128)}, u32[]{:S(2)}) copy-start(f32[2,160,896]{2,1,0:T(8,128)} %get-tuple-element.50) | copy-start | bytes 3440644
  594.3 3.0 copy-start.6
  594.3 4.0 copy-start.5
  594.3 5.0 copy-start.4

commit v2 on v1

v2 whole, which is shorter than its diff:
```python
import functools

import jax
import jax.numpy as jnp
from jax import lax
from jax.experimental import pallas as pl
from jax.experimental.pallas import tpu as pltpu
from jax.sharding import PartitionSpec as P

F32, BF16 = jnp.float32, jnp.bfloat16


def dot(a, b, contract):
    return lax.dot_general(a, b, (contract, ((), ())), preferred_element_type=F32)


def nn(a, b):
    return dot(a, b, ((1,), (0,)))


def nt(a, b):
    return dot(a, b, ((1,), (1,)))


def adamw(w, m, v, g):
    m = 0.9 * m + 0.1 * g
    v = 0.95 * v + 0.05 * g * g
    step = m * lax.rsqrt(v + 1e-8) + 0.1 * w
    return (w - 0.02 * step).astype(BF16), m, v


def normed(h):
    wide = h.astype(F32)
    scale = lax.rsqrt(jnp.mean(wide**2, -1, keepdims=True) + 1e-6)
    return (wide * scale).astype(BF16)


def normed_back(h, da):
    wide, da = h.astype(F32), da.astype(F32)
    scale = lax.rsqrt(jnp.mean(wide**2, -1, keepdims=True) + 1e-6)
    inner = jnp.mean(wide * da, -1, keepdims=True)
    return (da * scale - wide * (scale * scale * scale * inner)).astype(BF16)


def chain_kernel(tokens, x_ref, dy_ref, *refs):
    weights, refs = refs[:3], refs[3:]
    (a0, act0, dgate0, dup0, a1, act1, dgate1, dup1, dh1), refs = refs[:9], refs[9:]
    held, (gate_keep, up_keep, act_keep, dgate_keep, dup_keep, sem) = refs[:6], refs[6:]
    step = pl.program_id(0)
    wide = 256
    full = gate_keep.shape[1]

    def load(i):
        return pltpu.make_async_copy(weights[i % 3].at[i // 3], held[i], sem.at[i])

    @pl.when(step == 0)
    def _():
        for i in range(6):
            load(i).start()

    def need(i):
        @pl.when(step == 0)
        def _():
            load(i).wait()

    x, dy = x_ref[...], dy_ref[...]
    a = normed(x)
    a0[...] = a.T
    need(0)
    need(1)
    for c in range(0, full, wide):
        at = slice(c, c + wide)
        gate, up = nn(a, held[0][:, at]), nn(a, held[1][:, at])
        act = (jax.nn.silu(gate) * up).astype(BF16)
        gate_keep[:, at] = gate
        up_keep[:, at] = up
        act_keep[:, at] = act
        act0[at, :] = act.T
    need(2)
    h1 = (x.astype(F32) + nn(act_keep[...], held[2][...]).astype(BF16).astype(F32)).astype(BF16)
    a = normed(h1)
    a1[...] = a.T
    for i in (3, 4, 5):
        need(i)
    for c in range(0, full, wide):
        at = slice(c, c + wide)
        gate, up = nn(a, held[3][:, at]), nn(a, held[4][:, at])
        dact = nt(dy, held[5][at, :]).astype(BF16)
        act, dgate, dup = hidden_both(gate, up, dact)
        act1[at, :] = act.T
        dgate_keep[:, at] = dgate
        dup_keep[:, at] = dup
        dgate1[:, at] = dgate
        dup1[:, at] = dup
    da = nt(dgate_keep[...], held[3][...]).astype(BF16).astype(F32) + nt(dup_keep[...], held[4][...]).astype(BF16).astype(F32)
    dh = (dy.astype(F32) + normed_back(h1, da.astype(BF16)).astype(F32)).astype(BF16)
    dh1[...] = dh
    for c in range(0, full, wide):
        at = slice(c, c + wide)
        dact = nt(dh, held[2][at, :]).astype(BF16)
        _, dgate, dup = hidden_both(gate_keep[:, at], up_keep[:, at], dact)
        dgate0[:, at] = dgate
        dup0[:, at] = dup


def hidden_both(gate, up, dact):
    s = jax.nn.sigmoid(gate)
    dact = dact.astype(F32)
    gs = gate * s
    dup = dact * gs
    dgate = dact * up * (s + gs * (1.0 - s))
    return (gs * up).astype(BF16), dgate.astype(BF16), dup.astype(BF16)


def chain(x, dy, wg, wu, wd):
    tokens, d = x.shape
    full, tile = wg.shape[-1], 256
    across = lambda n: pl.BlockSpec((tile, n), lambda i: (i, 0))
    down = lambda n: pl.BlockSpec((n, tile), lambda i: (0, i))
    outs = [(d, True), (full, True), (full, False), (full, False)] * 2 + [(d, False)]
    return pl.pallas_call(
        functools.partial(chain_kernel, tokens),
        grid=(tokens // tile,),
        out_shape=[jax.ShapeDtypeStruct((n, tokens) if t else (tokens, n), BF16) for n, t in outs],
        in_specs=[across(d), across(d)] + [pl.BlockSpec(memory_space=pl.ANY)] * 3,
        out_specs=[down(n) if t else across(n) for n, t in outs],
        scratch_shapes=[pltpu.VMEM(one.shape[1:], BF16) for _ in range(2) for one in (wg, wu, wd)]
        + [pltpu.VMEM((tile, full), F32)] * 2
        + [pltpu.VMEM((tile, full), BF16)] * 3
        + [pltpu.SemaphoreType.DMA((6,))],
        compiler_params=pltpu.CompilerParams(vmem_limit_bytes=67_000_000, dimension_semantics=("arbitrary",)),
        cost_estimate=pl.CostEstimate(flops=18 * tokens * d * full, bytes_accessed=100_000_000, transcendentals=0),
        name="chain",
    )(x, dy, wg, wu, wd)


MESH = pl.DeviceIdType.MESH


def ring_kernel(order, shapes, *refs):
    n = len(order)
    take = iter(refs)
    operands = [(next(take), next(take)) for _ in range(n)]
    w, m, v = ([next(take) for _ in range(3)] for _ in range(3))
    w_new, m_new, v_new = ([next(take) for _ in range(3)] for _ in range(3))
    g, own, sib, rec = ([next(take) for _ in range(n)] for _ in range(4))
    (own_sem, sib_send, sib_recv, rs_send, rs_recv, ag_send, ag_recv, pass_send, pass_recv, load_sem, store_sem) = take

    me = lax.axis_index("dp")
    core, chip = me % 2, me // 2
    far = chip // 4
    place = chip * (1 - far) + far * (11 - chip)
    way = 1 - 2 * core

    def chip_at(p):
        p = (p + 16) % 8
        half = p // 4
        return p * (1 - half) + half * (11 - p)

    after = 2 * chip_at(place + way) + core
    before = 2 * chip_at(place - way) + core
    twin = me + way

    barrier = pltpu.get_barrier_semaphore()
    for other in (after, before, twin):
        pl.semaphore_signal(barrier, inc=1, device_id={"dp": other}, device_id_type=MESH)

    def own_copy(k, j):
        t = chip_at(place - way * (1 + j))
        return pltpu.make_async_copy(g[k].at[2 * t + core], own[k].at[j], own_sem.at[k, j])

    def sib_copy(k, j):
        t = chip_at(place + way * (1 + j))
        return pltpu.make_async_remote_copy(
            g[k].at[2 * t + 1 - core], sib[k].at[j], sib_send.at[k, j], sib_recv.at[k, j], {"dp": twin}, MESH
        )

    def ring_copy(k, j):
        return pltpu.make_async_remote_copy(
            own[k].at[j], rec[k].at[j], rs_send.at[k, j], rs_recv.at[k, j], {"dp": after}, MESH
        )

    def gather_copy(k, j, source=None):
        name, layer = order[k]
        there = w_new[name].at[layer, 2 * chip_at(place - way * j) + core]
        source = there if source is None else source
        return pltpu.make_async_remote_copy(source, there, ag_send.at[k, j], ag_recv.at[k, j], {"dp": after}, MESH)

    def twin_copy(k, j, source=None):
        name, layer = order[k]
        there = w_new[name].at[layer, 2 * chip_at(place - way * j) + core]
        source = there if source is None else source
        return pltpu.make_async_remote_copy(source, there, pass_send.at[k, j], pass_recv.at[k, j], {"dp": twin}, MESH)

    def over_columns(k, body):
        rows, columns = shapes[order[k][0]]
        wide = 256 if columns % 256 == 0 and rows < 100 else 128

        def piece(c, carry):
            body(pl.ds(pl.multiple_of(c * wide, wide), wide))
            return carry

        lax.fori_loop(0, columns // wide, piece, 0)

    def form(k, left, right, pieces, stage, kept_sem, in_sem, out_sem):
        down = order[k][0] == 2
        lhs, rhs = operands[k]
        tiles = g[k].shape[0] // stage.shape[1] if down else g[k].shape[2] // stage.shape[3]

        def get(i, slot):
            if down:
                size = pieces.shape[1]
                source = lhs.at[pl.ds(pl.multiple_of(i * size, size), size), :]
            else:
                size = pieces.shape[2]
                source = rhs.at[:, pl.ds(pl.multiple_of(i * size, size), size)]
            return pltpu.make_async_copy(source, pieces.at[slot], in_sem.at[slot])

        def put(i, slot):
            if down:
                size = stage.shape[1]
                target = g[k].at[pl.ds(pl.multiple_of(i * size, size), size)]
            else:
                size = stage.shape[3]
                target = g[k].at[:, :, pl.ds(pl.multiple_of(i * size, size), size)]
            return pltpu.make_async_copy(stage.at[slot], target, out_sem.at[slot])

        def prefetch():
            get(0, 0).start()
            get(1, 1).start()

        def run():
            @pl.loop(0, tiles)
            def _(i):
                slot = lax.rem(i, 2)
                get(i, slot).wait()
                if down:
                    made = nn(pieces[slot], right[...])
                else:
                    made = nn(left[...], pieces[slot])

                @pl.when(i >= 2)
                def _():
                    put(i, slot).wait()

                stage[slot] = made.reshape(stage.shape[1:]).astype(BF16)
                put(i, slot).start()

                @pl.when(i + 2 < tiles)
                def _():
                    get(i + 2, slot).start()

        def drain():
            put(0, 0).wait()
            put(1, 1).wait()

        return prefetch, run, drain

    def first(k):
        own_copy(k, 0).wait()
        sib_copy(k, 0).wait_recv()

        def add(at):
            own[k][0, :, at] = (own[k][0, :, at].astype(F32) + sib[k][0, :, at].astype(F32)).astype(BF16)

        over_columns(k, add)
        ring_copy(k, 0).start()

    def arrive(k, j):
        own_copy(k, j).wait()
        sib_copy(k, j).wait_recv()
        ring_copy(k, j - 1).wait_recv()

    def total(k, j, at):
        return own[k][j, :, at].astype(F32) + sib[k][j, :, at].astype(F32) + rec[k][j - 1, :, at].astype(F32)

    def onward(k, j):
        arrive(k, j)

        def add(at):
            own[k][j, :, at] = total(k, j, at).astype(BF16)

        over_columns(k, add)
        ring_copy(k, j).start()

    def forming(left, right, wide_in, wide_out, tall_in, tall_out, kept_sem, in_sem, out_sem):
        keep_right = lambda k: pltpu.make_async_copy(operands[k][1], right, kept_sem.at[0])
        keep_left = lambda k: pltpu.make_async_copy(operands[k][0], left, kept_sem.at[1])
        work = []
        for k in range(n):
            kind = int(order[k][0] == 2)
            buffers = (tall_in, tall_out) if kind else (wide_in, wide_out)
            work.append(form(k, left, right, *buffers, kept_sem, in_sem.at[kind], out_sem.at[kind]))
        keep_right(0).start()
        work[0][0]()
        keep_left(1).start()
        keep_right(0).wait()
        for k in range(n):
            work[k][1]()
            if k + 1 < n:
                if k == 0:
                    keep_right(3).start()
                if k == 2:
                    keep_left(4).start()
                work[k + 1][0]()
            work[k][2]()
            if k == 0:
                pl.semaphore_wait(barrier, 3)

            @pl.loop(0, 8)
            def _(j):
                own_copy(k, j).start()
                sib_copy(k, j).start()

            for older in range(k):
                onward(older, k - older)
            first(k)
            if k == 0:
                keep_left(1).wait()
            if k == 2:
                keep_right(3).wait()
            if k == 3:
                keep_left(4).wait()

    dma = pltpu.SemaphoreType.DMA
    pl.run_scoped(
        forming,
        pltpu.VMEM(operands[1][0].shape, BF16),
        pltpu.VMEM(operands[0][1].shape, BF16),
        pltpu.VMEM((2, operands[1][1].shape[0], WIDE), BF16),
        pltpu.VMEM((2, *g[1].shape[:2], WIDE), BF16),
        pltpu.VMEM((2, 2 * g[0].shape[1], operands[0][0].shape[1]), BF16),
        pltpu.VMEM((2, 2, *g[0].shape[1:]), BF16),
        dma((2,)),
        dma((2, 2)),
        dma((2, 2)),
    )

    def closing(*buffers):
        wv, mv, vv = buffers[:n], buffers[n : 2 * n], buffers[2 * n :]

        def loads(k):
            name, layer = order[k]
            return (
                pltpu.make_async_copy(w[name].at[layer, me], wv[k], load_sem.at[k, 0]),
                pltpu.make_async_copy(m[name].at[layer], mv[k], load_sem.at[k, 1]),
                pltpu.make_async_copy(v[name].at[layer], vv[k], load_sem.at[k, 2]),
            )

        def stores(k):
            name, layer = order[k]
            return (
                pltpu.make_async_copy(wv[k], w_new[name].at[layer, me], store_sem.at[k, 0]),
                pltpu.make_async_copy(mv[k], m_new[name].at[layer], store_sem.at[k, 1]),
                pltpu.make_async_copy(vv[k], v_new[name].at[layer], store_sem.at[k, 2]),
            )

        def finish(k):
            arrive(k, 7)
            for copy in loads(k):
                copy.wait()

            def step(at):
                grad = total(k, 7, at).astype(BF16).astype(F32)
                w_at, m_at, v_at = adamw(wv[k][:, at].astype(F32), mv[k][:, at], vv[k][:, at], grad)
                wv[k][:, at] = w_at
                mv[k][:, at] = m_at
                vv[k][:, at] = v_at

            over_columns(k, step)
            gather_copy(k, 0, wv[k]).start()
            twin_copy(k, 0, wv[k]).start()
            for copy in stores(k):
                copy.start()

        for k in range(n):
            for copy in loads(k):
                copy.start()

        @pl.loop(n, n + 14)
        def _(i):
            for k in range(n):
                j = i - k

                @pl.when(j <= 6)
                def _():
                    onward(k, j)

                @pl.when(j == 7)
                def _():
                    finish(k)

                @pl.when((j > 7) & (j < 14))
                def _():
                    gather_copy(k, j - 8).wait_recv()
                    gather_copy(k, j - 7).start()
                    twin_copy(k, j - 7).start()

                @pl.when(j == 14)
                def _():
                    gather_copy(k, 6).wait_recv()
                    twin_copy(k, 7).start()

        @pl.loop(0, 8)
        def _(j):
            for k in range(n):
                sib_copy(k, j).wait_send()
                twin_copy(k, j).wait()

        @pl.loop(0, 7)
        def _(j):
            for k in range(n):
                ring_copy(k, j).wait_send()
                gather_copy(k, j).wait_send()

        for k in range(n):
            for copy in stores(k):
                copy.wait()

    pl.run_scoped(closing, *(pltpu.VMEM(shapes[name], dtype) for dtype in (BF16, F32, F32) for name, _ in order))


ORDER = ((2, 1), (0, 1), (1, 1), (2, 0), (0, 0), (1, 0))
WIDE = 512


def ring_step(operands, w, m, v):
    n, shapes = len(ORDER), [one.shape[1:] for one in m]
    dma = pltpu.SemaphoreType.DMA
    scratch = [pltpu.VMEM((blocks, *shapes[name]), BF16) for blocks in (8, 8, 7) for name, _ in ORDER]
    scratch += [dma((n, 8))] * 3 + [dma((n, 7))] * 4 + [dma((n, 8))] * 2 + [dma((n, 3))] * 2
    anywhere = pl.BlockSpec(memory_space=pl.ANY)
    outs = [jax.ShapeDtypeStruct(one.shape, one.dtype) for one in (*w, *m, *v)]
    outs += [jax.ShapeDtypeStruct((16, *shapes[name]), BF16) for name, _ in ORDER]
    d, full, tokens = 16 * shapes[0][0], shapes[0][1], operands[0][1].shape[0]
    return pl.pallas_call(
        functools.partial(ring_kernel, ORDER, shapes),
        out_shape=outs,
        in_specs=[anywhere] * (2 * n + 9),
        out_specs=[anywhere] * len(outs),
        scratch_shapes=scratch,
        compiler_params=pltpu.CompilerParams(collective_id=0, has_side_effects=True, vmem_limit_bytes=67_000_000),
        cost_estimate=pl.CostEstimate(flops=12 * tokens * d * full, bytes_accessed=200_000_000, transcendentals=0),
        name="ring_step",
    )(*(one for pair in operands for one in pair), *w, *m, *v)[:9]


def solution(mesh):
    def body(x, dy, wg, wu, wd, mg, mu, md, vg, vu, vd):
        x, dy = x[0], dy[0]
        at0, actt0, dgate0, dup0, at1, actt1, dgate1, dup1, dh1 = chain(x, dy, wg, wu, wd)
        def blocks(one):
            return one.reshape(2, 16, -1, one.shape[-1])

        pairs = [(actt1, dy), (at1, dgate1), (at1, dup1), (actt0, dh1), (at0, dgate0), (at0, dup0)]
        new = ring_step(pairs, [blocks(one) for one in (wg, wu, wd)], [mg, mu, md], [vg, vu, vd])
        return tuple(one.reshape(2, -1, one.shape[-1]) for one in new[:3]) + tuple(new[3:])

    one, shard = P(("rep", "dp"), None, None), P(None, "dp", None)
    rep = P(None, None, None)
    outs = (P("rep", None, None),) * 3 + (P("rep", "dp", None),) * 6
    return jax.shard_map(body, mesh=mesh, in_specs=(one, one, rep, rep, rep) + (shard,) * 6, out_specs=outs, check_vma=False)
```

time: 608 us -> 468 us (0.77); the launches traced: 601 us -> 468 us
  matrix products: 277 us -> 0 us
  Pallas kernels: 271 us -> 438 us
  local copies, waits for them, and re-layouts: 42.2 us -> 29.9 us
  other arithmetic: 9.84 us -> 0 us
    dot_general x15 -> x0, matrix products: 277 us -> none  [dot(): lax.dot_general(a, b, (contract, ((), ())), preferred_element_type=F32)]
    pallas_call x1 -> x2, Pallas kernels: 271 us -> 438 us  [the longest x1 314 us: ring_step(): pl.pallas_call(functools.partial(ring_kernel, ORDER, shapes), out_shape=o...]
    unnamed x63 -> x21, local copies, waits for them, and re-layouts: 42.2 us -> 29.9 us
    add x1 -> x0, other arithmetic: 7.01 us -> none  [body(): dh1 = dy + normed_back(h1, da1)]
where the time goes in v2:
time: 468 us
  Pallas kernels  438 us (94%)
  local copies, waits for them, and re-layouts  29.9 us (6%)
    pallas_call x1, Pallas kernels, ring_step(): pl.pallas_call(functools.partial(ring_kernel, ORDER, shapes), out_shape=o...  314 us
    pallas_call x1, Pallas kernels, chain(): pl.pallas_call(functools.partial(chain_kernel, tokens), grid=(tokens // t...  123 us
    unnamed x21, local copies, waits for them, and re-layouts  29.9 us

profile of v2, /device:TPU:0, one launch (start us, length us, event | category | flops | bytes accessed | tf_op | source)
XLA Modules:
  0.0 468.1 jit_solution(9335189085347038834)
XLA Ops:
  0.6 123.1 %chain.1 = (bf16[896,2048]{1,0:T(8,128)(2,1)}, bf16[2560,2048]{1,0:T(8,128)(2,1)}, bf16[2048,2560]{1,0:T(8,128)(2,1)}, bf16[2048,2560]{1,0:T(8,128)(2,1)}, bf16[...) custom-call(bf16[2048,896]{1,0:T(8,128)(2,1)} %bitcast.14, ...), custom_call_target="tpu_custom_call" | custom-call | flops 84557168640 | bytes 100000000 | tf_op jit(solution)/shard_map/chain/pallas_call | solution.py:121
  123.8 314.4 %ring_step.1 = (bf16[2,16,56,2560]{3,2,1,0:T(8,128)(2,1)}, bf16[2,16,56,2560]{3,2,1,0:T(8,128)(2,1)}, bf16[2,16,160,896]{3,2,1,0:T(8,128)(2,1)}, f32[2,56,2560]{...) custom-call(bf16[2560,2048]{1,0:T(8,128)(2,1)} %get-tuple-element.27, ...), custom_call_target="tpu_custom_call" | custom-call | flops 56371445760 | bytes 200000000 | tf_op jit(solution)/shard_map/ring_step/pallas_call | solution.py:436
  438.2 7.9 %copy.29 = bf16[2,896,2560]{2,1,0:T(8,128)(2,1)} copy(bf16[2,896,2560]{2,1,0:T(8,128)(2,1)} %bitcast.10) | data formatting | bytes 18350080
  446.1 7.8 %copy.30 = bf16[2,896,2560]{2,1,0:T(8,128)(2,1)} copy(bf16[2,896,2560]{2,1,0:T(8,128)(2,1)} %bitcast.9) | data formatting | bytes 18350080
  453.9 0.0 copy-start.5
  453.9 0.0 copy-start.4
  453.9 8.1 %copy.31 = bf16[2,2560,896]{2,1,0:T(8,128)(2,1)} copy(bf16[2,2560,896]{2,1,0:T(8,128)(2,1)} %bitcast.8) | data formatting | bytes 18350080
  462.1 0.0 copy-done.5
  462.1 0.0 copy-start.3
  462.1 0.0 copy-start.2
  462.1 1.0 copy.32
  463.1 0.0 copy-done.4
  463.1 0.0 copy-start.1
  463.1 1.0 copy.33
  464.1 0.0 copy-done.3
  464.1 0.0 copy-start
  464.1 1.0 copy.34
  465.1 0.0 copy-done.2
  465.1 1.0 copy.35
  466.1 0.0 copy-done.1
  466.1 1.0 copy.36
  467.1 0.0 copy-done
  467.1 1.0 copy.37
Async XLA Ops:
  453.9 8.1 %copy-start.5 = (f32[2,56,2560]{2,1,0:T(8,128)S(1)}, f32[2,56,2560]{2,1,0:T(8,128)}, u32[]{:S(2)}) copy-start(f32[2,56,2560]{2,1,0:T(8,128)} %get-tuple-element.57) | copy-start | bytes 3440644
  453.9 9.2 %copy-start.4 = (f32[2,56,2560]{2,1,0:T(8,128)S(1)}, f32[2,56,2560]{2,1,0:T(8,128)}, u32[]{:S(2)}) copy-start(f32[2,56,2560]{2,1,0:T(8,128)} %get-tuple-element.58) | copy-start | bytes 3440644
  462.1 2.0 copy-start.3
  462.1 3.0 copy-start.2
  463.1 3.0 copy-start.1
  464.1 3.0 copy-start

commit v3 on v1

v3 whole, which is shorter than its diff:
```python
import functools

import jax
import jax.numpy as jnp
from jax import lax
from jax.experimental import pallas as pl
from jax.experimental.pallas import tpu as pltpu
from jax.sharding import PartitionSpec as P

F32, BF16 = jnp.float32, jnp.bfloat16


def dot(a, b, contract):
    return lax.dot_general(a, b, (contract, ((), ())), preferred_element_type=F32)


def nn(a, b):
    return dot(a, b, ((1,), (0,)))


def nt(a, b):
    return dot(a, b, ((1,), (1,)))


def adamw(w, m, v, g):
    m = 0.9 * m + 0.1 * g
    v = 0.95 * v + 0.05 * g * g
    step = m * lax.rsqrt(v + 1e-8) + 0.1 * w
    return (w - 0.02 * step).astype(BF16), m, v


def normed(h):
    wide = h.astype(F32)
    scale = lax.rsqrt(jnp.mean(wide**2, -1, keepdims=True) + 1e-6)
    return (wide * scale).astype(BF16)


def normed_back(h, da):
    wide, da = h.astype(F32), da.astype(F32)
    scale = lax.rsqrt(jnp.mean(wide**2, -1, keepdims=True) + 1e-6)
    inner = jnp.mean(wide * da, -1, keepdims=True)
    return (da * scale - wide * (scale * scale * scale * inner)).astype(BF16)


def chain_kernel(x_ref, dy_ref, *refs):
    weights, refs = refs[:3], refs[3:]
    (a0, act0, gate0, up0, h1_ref, a1, act1, dgate1, dup1), refs = refs[:9], refs[9:]
    held, (act_keep, sem) = refs[:6], refs[6:]
    step = pl.program_id(0)
    wide = 256
    full = act_keep.shape[1]

    def load(i):
        return pltpu.make_async_copy(weights[i % 3].at[i // 3], held[i], sem.at[i])

    @pl.when(step == 0)
    def _():
        for i in range(6):
            load(i).start()

    def need(i):
        @pl.when(step == 0)
        def _():
            load(i).wait()

    x, dy = x_ref[...], dy_ref[...]
    a = normed(x)
    a0[...] = a.T
    need(0)
    need(1)
    for c in range(0, full, wide):
        at = slice(c, c + wide)
        gate, up = nn(a, held[0][:, at]), nn(a, held[1][:, at])
        act = (jax.nn.silu(gate) * up).astype(BF16)
        gate0[:, at] = gate
        up0[:, at] = up
        act_keep[:, at] = act
        act0[at, :] = act.T
    need(2)
    h1 = (x.astype(F32) + nn(act_keep[...], held[2][...]).astype(BF16).astype(F32)).astype(BF16)
    h1_ref[...] = h1
    a = normed(h1)
    a1[...] = a.T
    for i in (3, 4, 5):
        need(i)
    for c in range(0, full, wide):
        at = slice(c, c + wide)
        gate, up = nn(a, held[3][:, at]), nn(a, held[4][:, at])
        dact = nt(dy, held[5][at, :]).astype(BF16)
        act, dgate, dup = hidden_both(gate, up, dact)
        act1[at, :] = act.T
        dgate1[:, at] = dgate
        dup1[:, at] = dup


def hidden_both(gate, up, dact):
    s = jax.nn.sigmoid(gate)
    dact = dact.astype(F32)
    gs = gate * s
    dup = dact * gs
    dgate = dact * up * (s + gs * (1.0 - s))
    return (gs * up).astype(BF16), dgate.astype(BF16), dup.astype(BF16)


TILE = 256


def chain(x, dy, wg, wu, wd):
    tokens, d = x.shape
    full = wg.shape[-1]
    across = lambda n: pl.BlockSpec((TILE, n), lambda i: (i, 0))
    down = lambda n: pl.BlockSpec((n, TILE), lambda i: (0, i))
    outs = [(d, True, BF16), (full, True, BF16), (full, False, F32), (full, False, F32), (d, False, BF16)]
    outs += [(d, True, BF16), (full, True, BF16), (full, False, BF16), (full, False, BF16)]
    return pl.pallas_call(
        chain_kernel,
        grid=(tokens // TILE,),
        out_shape=[jax.ShapeDtypeStruct((n, tokens) if t else (tokens, n), dtype) for n, t, dtype in outs],
        in_specs=[across(d), across(d)] + [pl.BlockSpec(memory_space=pl.ANY)] * 3,
        out_specs=[down(n) if t else across(n) for n, t, _ in outs],
        scratch_shapes=[pltpu.VMEM(one.shape[1:], BF16) for _ in range(2) for one in (wg, wu, wd)]
        + [pltpu.VMEM((TILE, full), BF16), pltpu.SemaphoreType.DMA((6,))],
        compiler_params=pltpu.CompilerParams(vmem_limit_bytes=67_000_000, dimension_semantics=("arbitrary",)),
        cost_estimate=pl.CostEstimate(flops=12 * tokens * d * full, bytes_accessed=130_000_000, transcendentals=0),
        name="chain",
    )(x, dy, wg, wu, wd)


MESH = pl.DeviceIdType.MESH


def ring_kernel(order, shapes, *refs):
    n, half = len(order), len(order) // 2
    take = iter(refs)
    actt1, dy, at1, dgate1, dup1, actt0, at0, gate0, up0, h1 = (next(take) for _ in range(10))
    w, m, v, w_flat = ([next(take) for _ in range(3)] for _ in range(4))
    w_new, m_new, v_new = ([next(take) for _ in range(3)] for _ in range(3))
    g = [next(take) for _ in range(n)]
    dh1, dgate0, dup0 = (next(take) for _ in range(3))
    operands = ((actt1, dy), (at1, dgate1), (at1, dup1), (actt0, dh1), (at0, dgate0), (at0, dup0))
    own, sib, rec, wv, mv, vv = ([next(take) for _ in range(half)] * 2 for _ in range(6))
    (own_sem, sib_send, sib_recv, rs_send, rs_recv, ag_send, ag_recv, pass_send, pass_recv, load_sem, store_sem) = (
        next(take) for _ in range(11)
    )
    ring_free, sib_free, wg1, wu1, wd0, whole_sem = take

    me = lax.axis_index("dp")
    core, chip = me % 2, me // 2
    far = chip // 4
    place = chip * (1 - far) + far * (11 - chip)
    way = 1 - 2 * core

    def chip_at(p):
        p = (p + 16) % 8
        half = p // 4
        return p * (1 - half) + half * (11 - p)

    after = 2 * chip_at(place + way) + core
    before = 2 * chip_at(place - way) + core
    twin = me + way

    barrier = pltpu.get_barrier_semaphore()
    for other in (after, before, twin):
        pl.semaphore_signal(barrier, inc=1, device_id={"dp": other}, device_id_type=MESH)

    def own_copy(k, j):
        t = chip_at(place - way * (1 + j))
        return pltpu.make_async_copy(g[k].at[2 * t + core], own[k].at[j], own_sem.at[k, j])

    def sib_copy(k, j):
        t = chip_at(place + way * (1 + j))
        return pltpu.make_async_remote_copy(
            g[k].at[2 * t + 1 - core], sib[k].at[j], sib_send.at[k, j], sib_recv.at[k, j], {"dp": twin}, MESH
        )

    def ring_copy(k, j):
        return pltpu.make_async_remote_copy(
            own[k].at[j], rec[k].at[j], rs_send.at[k, j], rs_recv.at[k, j], {"dp": after}, MESH
        )

    def gather_copy(k, j, source=None):
        name, layer = order[k]
        there = w_new[name].at[layer, 2 * chip_at(place - way * j) + core]
        source = there if source is None else source
        return pltpu.make_async_remote_copy(source, there, ag_send.at[k, j], ag_recv.at[k, j], {"dp": after}, MESH)

    def twin_copy(k, j, source=None):
        name, layer = order[k]
        there = w_new[name].at[layer, 2 * chip_at(place - way * j) + core]
        source = there if source is None else source
        return pltpu.make_async_remote_copy(source, there, pass_send.at[k, j], pass_recv.at[k, j], {"dp": twin}, MESH)

    def over_columns(k, body):
        rows, columns = shapes[order[k][0]]
        wide = 256 if columns % 256 == 0 and rows < 100 else 128

        def piece(c, carry):
            body(pl.ds(pl.multiple_of(c * wide, wide), wide))
            return carry

        lax.fori_loop(0, columns // wide, piece, 0)

    def loads(k):
        name, layer = order[k]
        return (
            pltpu.make_async_copy(w[name].at[layer, me], wv[k], load_sem.at[k, 0]),
            pltpu.make_async_copy(m[name].at[layer], mv[k], load_sem.at[k, 1]),
            pltpu.make_async_copy(v[name].at[layer], vv[k], load_sem.at[k, 2]),
        )

    def stores(k):
        name, layer = order[k]
        return (
            pltpu.make_async_copy(wv[k], w_new[name].at[layer, me], store_sem.at[k, 0]),
            pltpu.make_async_copy(mv[k], m_new[name].at[layer], store_sem.at[k, 1]),
            pltpu.make_async_copy(vv[k], v_new[name].at[layer], store_sem.at[k, 2]),
        )

    def total(k, j, at):
        return own[k][j, :, at].astype(F32) + sib[k][j, :, at].astype(F32) + rec[k][j - 1, :, at].astype(F32)

    def arrive(k, j):
        own_copy(k, j).wait()
        sib_copy(k, j).wait_recv()
        ring_copy(k, j - 1).wait_recv()

    def first(k):
        own_copy(k, 0).wait()
        sib_copy(k, 0).wait_recv()

        def add(at):
            own[k][0, :, at] = (own[k][0, :, at].astype(F32) + sib[k][0, :, at].astype(F32)).astype(BF16)

        over_columns(k, add)
        if k >= half:
            pl.semaphore_wait(ring_free.at[k - half], 1)
        ring_copy(k, 0).start()

    def onward(k, j):
        arrive(k, j)

        def add(at):
            own[k][j, :, at] = total(k, j, at).astype(BF16)

        over_columns(k, add)
        ring_copy(k, j).start()

    def finish(k):
        arrive(k, 7)
        for copy in loads(k):
            copy.wait()

        def step(at):
            grad = total(k, 7, at).astype(BF16).astype(F32)
            w_at, m_at, v_at = adamw(wv[k][:, at].astype(F32), mv[k][:, at], vv[k][:, at], grad)
            wv[k][:, at] = w_at
            mv[k][:, at] = m_at
            vv[k][:, at] = v_at

        over_columns(k, step)
        if k < half:
            pl.semaphore_signal(ring_free.at[k], inc=1, device_id={"dp": before}, device_id_type=MESH)
            pl.semaphore_signal(sib_free.at[k], inc=1, device_id={"dp": twin}, device_id_type=MESH)
        gather_copy(k, 0, wv[k]).start()
        twin_copy(k, 0, wv[k]).start()
        for copy in stores(k):
            copy.start()

    def hand_on(k, j):
        gather_copy(k, j - 8).wait_recv()
        gather_copy(k, j - 7).start()
        twin_copy(k, j - 7).start()

    def last(k):
        gather_copy(k, 6).wait_recv()
        twin_copy(k, 7).start()

    def service(k, j, least=0):
        for low, high, act in ((0, 0, lambda: first(k)), (1, 6, lambda: onward(k, j)), (7, 7, lambda: finish(k))):
            if high >= least:
                pl.when((j >= low) & (j <= high))(act)
        pl.when((j >= 8) & (j <= 13))(lambda: hand_on(k, j))
        pl.when(j == 14)(lambda: last(k))

    def make_room(k):
        old = k - half

        @pl.loop(0, 7)
        def _(j):
            ring_copy(old, j).wait_send()

        gather_copy(old, 0).wait_send()
        twin_copy(old, 0).wait_send()
        for copy in stores(old):
            copy.wait()
        for copy in loads(k):
            copy.start()
        pl.semaphore_wait(sib_free.at[old], 1)

    def send_off(k, low, high):
        @pl.loop(low, high)
        def _(j):
            own_copy(k, j).start()
            sib_copy(k, j).start()

    def form(k, left, right, pieces, stage, in_sem, out_sem):
        down = order[k][0] == 2
        lhs, rhs = operands[k]
        tiles = 8 if down else g[k].shape[2] // stage.shape[3]

        def target_of(i):
            turn = i // 2
            step = way * (1 + turn) * (2 * (i % 2) - 1) * (1 - i // 7)
            return chip_at(place + step)

        def get(i, slot):
            if down:
                size = pieces.shape[1]
                source = lhs.at[pl.ds(pl.multiple_of(target_of(i) * size, size), size), :]
            else:
                size = pieces.shape[2]
                source = rhs.at[:, pl.ds(pl.multiple_of(i * size, size), size)]
            return pltpu.make_async_copy(source, pieces.at[slot], in_sem.at[slot])

        def put(i, slot):
            if down:
                target = g[k].at[pl.ds(2 * target_of(i), 2)]
            else:
                size = stage.shape[3]
                target = g[k].at[:, :, pl.ds(pl.multiple_of(i * size, size), size)]
            return pltpu.make_async_copy(stage.at[slot], target, out_sem.at[slot])

        def prefetch():
            get(0, 0).start()
            get(1, 1).start()

        def tile(i, settled):
            slot = lax.rem(i, 2)
            get(i, slot).wait()
            made = nn(pieces[slot], right[...]) if down else nn(left[...], pieces[slot])
            if not settled:

                @pl.when(i >= 2)
                def _():
                    put(i, slot).wait()

            stage[slot] = made.reshape(stage.shape[1:]).astype(BF16)
            put(i, slot).start()

            @pl.when(i + 2 < tiles)
            def _():
                get(i + 2, slot).start()

        def settle():
            put(0, 0).wait()
            put(1, 1).wait()

        return prefetch, tile, settle, tiles

    def forming(base, between, left, right, wide_in, wide_out, tall_in, tall_out, kept_sem, in_sem, out_sem):
        keep_right = pltpu.make_async_copy(operands[base][1], right, kept_sem.at[0])
        keep_left = pltpu.make_async_copy(operands[base + 1][0], left, kept_sem.at[1])
        work = []
        for k in range(base, base + half):
            kind = int(order[k][0] == 2)
            buffers = (tall_in, tall_out) if kind else (wide_in, wide_out)
            work.append(form(k, left, right, *buffers, in_sem.at[kind], out_sem.at[kind]))
        keep_right.start()
        work[0][0]()
        keep_left.start()
        work[1][0]()
        keep_right.wait()
        if base:
            make_room(base)
        else:
            for k in range(half):
                for copy in loads(k):
                    copy.start()
            for i in range(3):
                whole(i).start()

        @pl.loop(0, 4)
        def _(turn):
            work[0][1](2 * turn, True)
            work[0][1](2 * turn + 1, True)
            work[0][2]()
            if not base:

                @pl.when(turn == 0)
                def _():
                    pl.semaphore_wait(barrier, 3)

            own_copy(base, turn).start()
            sib_copy(base, turn).start()

            @pl.when(turn == 1)
            def _():
                between(0)
                first(base)

            @pl.when(turn == 3)
            def _():
                between(1)
                onward(base, 1)

        send_off(base, 4, 8)
        keep_left.wait()

        @pl.loop(0, work[1][3])
        def _(i):
            work[1][1](i, False)
            pl.when(i == 1)(lambda: between(2))

            @pl.when(i == 3)
            def _():
                between(3)
                onward(base, 2)

        work[1][2]()
        work[2][0]()
        if base:
            make_room(base + 1)
        send_off(base + 1, 0, 8)

        @pl.loop(0, work[2][3])
        def _(i):
            work[2][1](i, False)

            @pl.when(i == 0)
            def _():
                between(4)
                onward(base, 3)
                first(base + 1)

            pl.when(i == 2)(lambda: between(5))

            @pl.when(i == 3)
            def _():
                between(6)
                onward(base, 4)
                onward(base + 1, 1)

        work[2][2]()
        if base:
            make_room(base + 2)
        send_off(base + 2, 0, 8)

    dma = pltpu.SemaphoreType.DMA
    formers = (
        pltpu.VMEM(at1.shape, BF16),
        pltpu.VMEM(dy.shape, BF16),
        pltpu.VMEM((2, dgate1.shape[0], WIDE), BF16),
        pltpu.VMEM((2, *g[1].shape[:2], WIDE), BF16),
        pltpu.VMEM((2, 2 * g[0].shape[1], actt1.shape[1]), BF16),
        pltpu.VMEM((2, 2, *g[0].shape[1:]), BF16),
        dma((2,)),
        dma((2, 2)),
        dma((2, 2)),
    )

    def round_of(i, base):
        service(base, 5 + i, 5)
        service(base + 1, 2 + i, 2)
        service(base + 2, i)

    def whole(i):
        layer, held = ((1, wg1), (1, wu1), (0, wd0))[i]
        return pltpu.make_async_copy(w_flat[i].at[layer], held, whole_sem.at[i])

    def backward(*buffers):
        arrays, outs = (dgate1, dup1, gate0, up0, h1, dy), (dgate0, dup0, dh1)
        slots, stage, (in_sem, out_sem) = buffers[:6], buffers[6:9], buffers[9:]
        rows = stage[0].shape[0]
        tiles = dy.shape[0] // rows

        def get(i, slot, b):
            source = arrays[b].at[pl.ds(pl.multiple_of(i * rows, rows), rows), :]
            return pltpu.make_async_copy(source, slots[b].at[slot], in_sem.at[slot, b])

        def put(i, b):
            target = outs[b].at[pl.ds(pl.multiple_of(i * rows, rows), rows), :]
            return pltpu.make_async_copy(stage[b], target, out_sem.at[b])

        for i in range(2):
            for b in range(6):
                get(i, i, b).start()
        for i in range(3):
            whole(i).wait()

        @pl.loop(0, tiles)
        def _(i):
            slot = lax.rem(i, 2)
            round_of(i, 0)
            for b in range(6):
                get(i, slot, b).wait()
            da = nt(slots[0][slot], wg1[...]).astype(BF16).astype(F32) + nt(slots[1][slot], wu1[...]).astype(BF16).astype(F32)
            back = normed_back(slots[4][slot], da.astype(BF16)).astype(F32)
            dh = (slots[5][slot].astype(F32) + back).astype(BF16)

            @pl.when(i > 0)
            def _():
                for b in range(3):
                    put(i, b).wait()

            stage[2][...] = dh
            put(i, 2).start()
            wide = 256
            for c in range(0, wd0.shape[0], wide):
                at = slice(c, c + wide)
                dact = nt(dh, wd0[at, :]).astype(BF16)
                _, dgate, dup = hidden_both(slots[2][slot, :, at], slots[3][slot, :, at], dact)
                stage[0][:, at] = dgate
                stage[1][:, at] = dup
            put(i, 0).start()
            put(i, 1).start()

            @pl.when(i + 2 < tiles)
            def _():
                for b in range(6):
                    get(i + 2, slot, b).start()

        for b in range(3):
            put(0, b).wait()

    def leftover(s):
        for k, j in ((0, 13 + s), (1, 10 + s), (2, 8 + s)):
            if j < 14:
                hand_on(k, j)
            elif j == 14:
                last(k)

    pl.run_scoped(functools.partial(forming, 0, lambda s: None), *formers)
    pl.run_scoped(
        backward,
        *(pltpu.VMEM((2, BACK, one.shape[1]), one.dtype) for one in (dgate1, dup1, gate0, up0, h1, dy)),
        *(pltpu.VMEM((BACK, one.shape[1]), BF16) for one in (dgate0, dup0, dh1)),
        dma((2, 6)),
        dma((3,)),
    )
    pl.run_scoped(functools.partial(forming, half, leftover), *formers)

    @pl.loop(0, 15)
    def _(i):
        round_of(i, half)

    @pl.loop(0, 8)
    def _(j):
        for k in range(n):
            sib_copy(k, j).wait_send()
            twin_copy(k, j).wait_recv()

    @pl.loop(0, 7)
    def _(j):
        for k in range(half):
            ring_copy(half + k, j).wait_send()
            gather_copy(half + k, j).wait_send()
            twin_copy(half + k, j).wait_send()

    @pl.loop(1, 7)
    def _(j):
        for k in range(half):
            gather_copy(k, j).wait_send()
            twin_copy(k, j).wait_send()

    for k in range(n):
        twin_copy(k, 7).wait_send()
    for k in range(half, n):
        for copy in stores(k):
            copy.wait()


ORDER = ((2, 1), (0, 1), (1, 1), (2, 0), (0, 0), (1, 0))
WIDE = 512
BACK = 256


def ring_step(operands, w, m, v):
    n, half, shapes = len(ORDER), len(ORDER) // 2, [one.shape[1:] for one in m]
    dma = pltpu.SemaphoreType.DMA
    scratch = [pltpu.VMEM((blocks, *shapes[name]), BF16) for blocks in (8, 8, 7) for name, _ in ORDER[:half]]
    scratch += [pltpu.VMEM(shapes[name], dtype) for dtype in (BF16, F32, F32) for name, _ in ORDER[:half]]
    scratch += [dma((n, 8))] * 3 + [dma((n, 7))] * 4 + [dma((n, 8))] * 2 + [dma((n, 3))] * 2
    scratch += [pltpu.SemaphoreType.REGULAR((half,))] * 2
    scratch += [pltpu.VMEM(one.shape[1:], BF16) for one in w] + [dma((3,))]
    anywhere = pl.BlockSpec(memory_space=pl.ANY)
    by_device = [one.reshape(2, 16, *shape) for one, shape in zip(w, shapes)]
    outs = [jax.ShapeDtypeStruct(one.shape, one.dtype) for one in (*by_device, *m, *v)]
    outs += [jax.ShapeDtypeStruct((16, *shapes[name]), BF16) for name, _ in ORDER]
    d, full, tokens = 16 * shapes[0][0], shapes[0][1], operands[1].shape[0]
    outs += [jax.ShapeDtypeStruct((tokens, width), BF16) for width in (d, full, full)]
    return pl.pallas_call(
        functools.partial(ring_kernel, ORDER, shapes),
        out_shape=outs,
        in_specs=[anywhere] * (len(operands) + 12),
        out_specs=[anywhere] * len(outs),
        scratch_shapes=scratch,
        compiler_params=pltpu.CompilerParams(collective_id=0, has_side_effects=True, vmem_limit_bytes=67_000_000),
        cost_estimate=pl.CostEstimate(flops=18 * tokens * d * full, bytes_accessed=250_000_000, transcendentals=0),
        name="ring_step",
    )(*operands, *by_device, *m, *v, *w)[:9]


def settle_kernel(*refs):
    ins, outs, held, (in_sem, out_sem) = refs[:3], refs[3:6], refs[6:9], refs[9:]
    pieces = [(i, layer, c) for layer in range(2) for c in range(4) for i in range(3)]

    def get(n):
        i, layer, c = pieces[n]
        at = (layer, slice(4 * c, 4 * c + 4))
        return pltpu.make_async_copy(ins[i].at[at], held[i].at[at], in_sem.at[n])

    def put(n):
        i, layer, c = pieces[n]
        at = (layer, slice(4 * c, 4 * c + 4))
        return pltpu.make_async_copy(held[i].at[at], outs[i].at[at], out_sem.at[n])

    for n in range(len(pieces)):
        get(n).start()
    for n in range(len(pieces)):
        get(n).wait()
        put(n).start()
    for n in range(len(pieces)):
        put(n).wait()


def settle(w):
    anywhere = pl.BlockSpec(memory_space=pl.ANY)
    return pl.pallas_call(
        settle_kernel,
        out_shape=[jax.ShapeDtypeStruct(one.shape, one.dtype) for one in w],
        in_specs=[anywhere] * 3,
        out_specs=[anywhere] * 3,
        scratch_shapes=[pltpu.VMEM(one.shape, BF16) for one in w] + [pltpu.SemaphoreType.DMA((24,))] * 2,
        compiler_params=pltpu.CompilerParams(vmem_limit_bytes=67_000_000),
        cost_estimate=pl.CostEstimate(flops=10_000_000, bytes_accessed=55_000_000, transcendentals=0),
        name="settle",
    )(*w)


def solution(mesh):
    def body(x, dy, wg, wu, wd, mg, mu, md, vg, vu, vd):
        x, dy = x[0], dy[0]
        at0, actt0, gate0, up0, h1, at1, actt1, dgate1, dup1 = chain(x, dy, wg, wu, wd)
        operands = (actt1, dy, at1, dgate1, dup1, actt0, at0, gate0, up0, h1)
        new = ring_step(operands, (wg, wu, wd), (mg, mu, md), (vg, vu, vd))
        return tuple(one.reshape(2, -1, one.shape[-1]) for one in settle(new[:3])) + tuple(new[3:])

    one, shard = P(("rep", "dp"), None, None), P(None, "dp", None)
    rep = P(None, None, None)
    outs = (P("rep", None, None),) * 3 + (P("rep", "dp", None),) * 6
    return jax.shard_map(body, mesh=mesh, in_specs=(one, one, rep, rep, rep) + (shard,) * 6, out_specs=outs, check_vma=False)
```

time: 608 us -> 430 us (0.71); the launches traced: 601 us -> 430 us
  matrix products: 277 us -> 0 us
  Pallas kernels: 271 us -> 420 us
  local copies, waits for them, and re-layouts: 42.2 us -> 8.96 us
  other arithmetic: 9.84 us -> 0 us
    dot_general x15 -> x0, matrix products: 277 us -> none  [dot(): lax.dot_general(a, b, (contract, ((), ())), preferred_element_type=F32)]
    pallas_call x1 -> x3, Pallas kernels: 271 us -> 420 us  [the longest x1 318 us: ring_step(): pl.pallas_call(functools.partial(ring_kernel, ORDER, shapes), out_shape=o...]
    unnamed x63 -> x14, local copies, waits for them, and re-layouts: 42.2 us -> 8.96 us
    add x1 -> x0, other arithmetic: 7.01 us -> none  [body(): dh1 = dy + normed_back(h1, da1)]
where the time goes in v3:
time: 430 us
  Pallas kernels  420 us (98%)
  local copies, waits for them, and re-layouts  8.96 us (2%)
    pallas_call x1, Pallas kernels, ring_step(): pl.pallas_call(functools.partial(ring_kernel, ORDER, shapes), out_shape=o...  318 us
    pallas_call x1, Pallas kernels, chain(): pl.pallas_call(chain_kernel, grid=(tokens // TILE,), out_shape=[jax.Shape...  83.3 us
    pallas_call x1, Pallas kernels, settle(): pl.pallas_call(settle_kernel, out_shape=[jax.ShapeDtypeStruct(one.shape,...  18.7 us
    unnamed x14, local copies, waits for them, and re-layouts  8.96 us

profile of v3, /device:TPU:0, one launch (start us, length us, event | category | flops | bytes accessed | tf_op | source)
XLA Modules:
  0.0 430.1 jit_solution(2268911799046140539)
XLA Ops:
  0.6 83.3 %chain.1 = (bf16[896,2048]{1,0:T(8,128)(2,1)}, bf16[2560,2048]{1,0:T(8,128)(2,1)}, f32[2048,2560]{1,0:T(8,128)}, f32[2048,2560]{1,0:T(8,128)}, bf16[2048,896]{1,...) custom-call(bf16[2048,896]{1,0:T(8,128)(2,1)} %bitcast.14, ...), custom_call_target="tpu_custom_call" | custom-call | flops 56371445760 | bytes 130000000 | tf_op jit(solution)/shard_map/chain/pallas_call | solution.py:115
  83.9 318.4 %ring_step.1 = (bf16[2,16,56,2560]{3,2,1,0:T(8,128)(2,1)}, bf16[2,16,56,2560]{3,2,1,0:T(8,128)(2,1)}, bf16[2,16,160,896]{3,2,1,0:T(8,128)(2,1)}, f32[2,56,2560]{...) custom-call(bf16[2560,2048]{1,0:T(8,128)(2,1)} %get-tuple-element.30, ...), custom_call_target="tpu_custom_call" | custom-call | flops 84557168640 | bytes 250000000 | tf_op jit(solution)/shard_map/ring_step/pallas_call | solution.py:591
  402.3 18.7 %settle.1 = (bf16[2,16,56,2560]{3,2,1,0:T(8,128)(2,1)}, bf16[2,16,56,2560]{3,2,1,0:T(8,128)(2,1)}, bf16[2,16,160,896]{3,2,1,0:T(8,128)(2,1)}) custom-call(bf16[2,16,56,2560]{3,2,1,0:T(8,128)(2,1)} %get-tuple-element.39.refs_0_, bf16[2,16,56,2560]{3,2,1,0:T(8,128)(2,1)} %get-tuple-element.40.refs_1_, bf16[2,16,160,896]{3,2,1,0:T(8,128)(2,1)} %get-tuple-element.41.refs_2_), custom_call_target="tpu_custom_call" | custom-call | flops 10000000 | bytes 55000000 | tf_op jit(solution)/shard_map/settle/pallas_call | solution.py:628
  421.1 0.0 copy-start.3
  421.1 0.0 copy-start.2
  421.1 2.5 copy.26
  423.6 0.0 copy-start.1
  423.6 2.4 copy.27
  426.0 0.0 copy-done.3
  426.0 0.0 copy-start
  426.0 1.0 copy.28
  427.0 0.0 copy-done.2
  427.0 1.0 copy.29
  428.0 0.0 copy-done.1
  428.0 1.0 copy.30
  429.0 0.0 copy-done
  429.0 1.0 copy.31
Async XLA Ops:
  421.1 5.0 %copy-start.3 = (f32[2,160,896]{2,1,0:T(8,128)S(1)}, f32[2,160,896]{2,1,0:T(8,128)}, u32[]{:S(2)}) copy-start(f32[2,160,896]{2,1,0:T(8,128)} %get-tuple-element.65) | copy-start | bytes 3440644
  421.1 6.0 %copy-start.2 = (f32[2,56,2560]{2,1,0:T(8,128)S(1)}, f32[2,56,2560]{2,1,0:T(8,128)}, u32[]{:S(2)}) copy-start(f32[2,56,2560]{2,1,0:T(8,128)} %get-tuple-element.66) | copy-start | bytes 3440644
  423.6 4.5 %copy-start.1 = (f32[2,56,2560]{2,1,0:T(8,128)S(1)}, f32[2,56,2560]{2,1,0:T(8,128)}, u32[]{:S(2)}) copy-start(f32[2,56,2560]{2,1,0:T(8,128)} %get-tuple-element.67) | copy-start | bytes 3440644
  426.0 3.0 copy-start
